TPU v7x, 256 devices: a whole 4x4x8 slice. The times are simulated.
256 devices in a mesh: vert: 256 (over z, x, y, core).
Axes of the slice: x: 4, y: 4, z: 8, core: 2. Of those that a mesh axis runs over, the one named last changes fastest.
Arguments:
- feats: bfloat16 [524288, 128], P('vert'), may hold values from -6 to 6
- w_self: bfloat16 [128, 256], replicated, may hold values from -0.5 to 0.5
- w_neigh: bfloat16 [128, 256], replicated, may hold values from -0.5 to 0.5
- bias: float32 [256], replicated, may hold values from -0.6 to 0.6
- cotangent: bfloat16 [524288, 256], P('vert'), may hold values from -24 to 24
- send_rows: int32 [256, 256, 8], P('vert'), may hold values from 0 to 2047
- hub_ids: int32 [368], replicated, may hold values from 0 to 524287, as said below
- edge_src: int32 [256, 16384], P('vert'), may hold values from 0 to 4463, as said below
- edge_dst: int32 [256, 16384], P('vert'), may hold values from 0 to 2047, never falling along the last dimension, each value on 1 to 64 neighbouring positions
- edge_count: int32 [256], P('vert'), may hold values from 1 to 16384, 1677721 in all
Outputs:
- output: bfloat16 [524288, 256], P('vert')
- grad_feats: bfloat16 [524288, 128], P('vert')
- grad_w_self: float32 [128, 256], replicated
- grad_w_neigh: float32 [128, 256], replicated
- grad_bias: float32 [256], replicated
Inputs may be any that keep to these rules, and one draw needn't show every extreme that they name: edge_src[d, e] indexes block d's source table: values below 2048 are own rows, values from 2048 to 4095 are halo slots (owner p = (value - 2048) // 8, slot c = (value - 2048) % 8), higher values are hubs (index value - 2048 - 256*8 into hub_ids). hub_ids is strictly ascending; no device's id range holds more than 8 hubs, some device's range holds exactly 8, and every device's range holds at least one.
All inputs are finite; a program needn't handle non-finite values.
Results may differ from a plain program's by a relative error of at most 0.0055.
Values may be sent and summed in bfloat16 or wider, within the bound.
A program may use at most 64 MiB of HBM per device.

v0:
```python
import jax
import jax.numpy as jnp
from jax import lax
from jax.sharding import PartitionSpec as P

HUB_MOST = 8


def together(arrays, axis):
    line, at, outs = jnp.concatenate([a.reshape(-1) for a in arrays]), 0, []
    total = lax.psum(line, axis)
    for a in arrays:
        outs.append(total[at : at + a.size].reshape(a.shape))
        at += a.size
    return tuple(outs)


def silu_slope(linear):
    logistic = jax.nn.sigmoid(linear)
    return logistic * (1.0 + linear * (1.0 - logistic))


def body(
    feats, w_self, w_neigh, bias, cotangent, send_rows, hub_ids, edge_src, edge_dst, edge_count
):
    local_rows, feat_width = feats.shape
    peer_count = lax.axis_size("vert")
    own_index = lax.axis_index("vert")
    send_plan = send_rows[0]
    slot_count = send_plan.shape[1]
    hub_total = hub_ids.shape[0]
    edge_from = edge_src[0]
    edge_to = edge_dst[0]
    is_real = lax.iota(jnp.int32, edge_from.shape[0]) < edge_count[0]
    drop_to = jnp.where(is_real, edge_to, local_rows)
    degree = jax.ops.segment_sum(is_real.astype(jnp.float32), drop_to, num_segments=local_rows)
    inverse = 1.0 / jnp.maximum(degree, 1.0)
    hub_owner = hub_ids // local_rows
    hub_local = hub_ids - hub_owner * local_rows
    table_rows = local_rows + peer_count * slot_count + hub_total
    hub_count = jax.ops.segment_sum(jnp.ones_like(hub_owner), hub_owner, num_segments=peer_count)
    hub_first = jnp.cumsum(hub_count) - hub_count
    column = lax.iota(jnp.int32, HUB_MOST)
    padded = jnp.concatenate([hub_local, jnp.zeros((HUB_MOST,), jnp.int32)])
    own_hubs = lax.dynamic_slice_in_dim(padded, hub_first[own_index], HUB_MOST)
    own_hubs = jnp.where(column < hub_count[own_index], own_hubs, 0)
    sent_rows = jnp.concatenate(
        [send_plan, jnp.broadcast_to(own_hubs[None, :], (peer_count, HUB_MOST))], axis=1
    )
    arrived = lax.all_to_all(feats[sent_rows], "vert", split_axis=0, concat_axis=0, tiled=True)
    slot_depth = slot_count + HUB_MOST
    halo_block = arrived[:, :slot_count]
    hub_offset = lax.iota(jnp.int32, hub_total) - hub_first[hub_owner]
    hub_place = hub_owner * slot_depth + slot_count + hub_offset
    hub_rows = arrived.reshape(-1, feat_width)[hub_place]
    remote = jnp.concatenate([halo_block.reshape(-1, feat_width), hub_rows], axis=0)
    source_table = jnp.concatenate([feats, remote], axis=0)
    summed = jax.ops.segment_sum(
        source_table[edge_from].astype(jnp.float32), drop_to, num_segments=local_rows
    )
    mean_rows = (summed * inverse[:, None]).astype(jnp.bfloat16)
    linear = jnp.dot(feats, w_self, preferred_element_type=jnp.float32)
    linear = linear + jnp.dot(mean_rows, w_neigh, preferred_element_type=jnp.float32) + bias
    output = jax.nn.silu(linear).astype(jnp.bfloat16)
    grad_linear = (cotangent.astype(jnp.float32) * silu_slope(linear)).astype(jnp.bfloat16)
    contracting = (((0,), (0,)), ((), ()))
    self_term = lax.dot_general(feats, grad_linear, contracting, preferred_element_type=jnp.float32)
    neigh_term = lax.dot_general(
        mean_rows, grad_linear, contracting, preferred_element_type=jnp.float32
    )
    bias_term = jnp.sum(grad_linear.astype(jnp.float32), axis=0)
    grad_w_self, grad_w_neigh, grad_bias = together((self_term, neigh_term, bias_term), "vert")
    own_grad = jnp.dot(grad_linear, w_self.T, preferred_element_type=jnp.float32)
    spread = jnp.dot(grad_linear, w_neigh.T, preferred_element_type=jnp.float32) * inverse[:, None]
    drop_from = jnp.where(is_real, edge_from, table_rows)
    back_table = jax.ops.segment_sum(spread[edge_to], drop_from, num_segments=table_rows)
    own_grad = own_grad + back_table[:local_rows]
    halo_edge = local_rows + peer_count * slot_count
    halo_back = back_table[local_rows:halo_edge].reshape(peer_count, slot_count, feat_width)
    hub_back = back_table[halo_edge:]
    slot_of_hub = hub_owner * HUB_MOST + hub_offset
    hub_slots = jax.ops.segment_sum(hub_back, slot_of_hub, num_segments=peer_count * HUB_MOST)
    outgoing = jnp.concatenate(
        [halo_back, hub_slots.reshape(peer_count, HUB_MOST, feat_width)], axis=1
    )
    returned = lax.all_to_all(
        outgoing.astype(jnp.bfloat16), "vert", split_axis=0, concat_axis=0, tiled=True
    ).astype(outgoing.dtype)
    own_grad = own_grad + jax.ops.segment_sum(
        returned.reshape(-1, feat_width), sent_rows.reshape(-1), num_segments=local_rows
    )
    return (output, own_grad.astype(jnp.bfloat16), grad_w_self, grad_w_neigh, grad_bias)


def solution(mesh):
    in_specs = (
        P("vert", None),
        P(),
        P(),
        P(),
        P("vert", None),
        P("vert", None, None),
        P(),
        P("vert", None),
        P("vert", None),
        P("vert"),
    )
    out_specs = (P("vert", None), P("vert", None), P(), P(), P())
    return jax.shard_map(body, mesh=mesh, in_specs=in_specs, out_specs=out_specs, check_vma=False)
```

profile of v0, /device:TPU:2, one launch (start us, length us, event | category | flops | bytes accessed | tf_op | source)
XLA Modules:
  0.0 788.9 jit_solution(5810602669724814307)
XLA Ops:
  7.2 0.8 compare_select_fusion.6
  8.0 3.8 scatter_custom_fusion
  11.8 0.6 dynamic_slice.9
  12.4 0.3 reduce-window.9
  13.0 0.6 dynamic_slice.10
  14.9 2.8 gather_fusion.1
  18.4 0.7 compare_select_fusion.7
  19.5 15.0 %gather_fusion = bf16[4096,128]{1,0:T(8,128)(2,1)} fusion(bf16[2048,128]{1,0:T(8,128)(2,1)S(1)} %copy-done.1, s32[4096]{0:T(1024)S(1)} %broadcast_clamp_fusion.2), kind=kCustom, calls=%fused_computation | custom fusion | bytes 2113536 | tf_op jit(solution)/shard_map/gather | solution.py:50
  34.6 14.7 %all-to-all-start = ((bf16[256,16,128]{2,1,0:T(8,128)(2,1)}), bf16[256,16,128]{2,1,0:T(8,128)(2,1)S(1)}, u32[]{:S(2)}, u32[]{:S(2)}) async-start(bf16[256,16,128]{2,1,0:T(8,128)(2,1)} %bitcast.8), calls=%async_computation | async-start | bytes 2097152 | tf_op jit(solution)/shard_map/all_to_all | solution.py:50
  50.0 0.2 compare_select_fusion
  50.5 87.5 %scatter_custom_fusion.2 = f32[2048]{0:T(1024)S(1)} fusion(s32[16384]{0:T(1024)S(1)} %bitcast.56, f32[16384]{0:T(1024)S(1)} %fusion.13, f32[]{:T(128)} %constant.15.clone.1), kind=kCustom, calls=%fused_computation.56 | custom fusion | flops 16384 | bytes 8196 | tf_op jit(solution)/shard_map/scatter-add | solution.py:36
  138.1 1.8 fusion.22
  139.9 1.4 gather_fusion.2
  141.5 138.0 %scatter_custom_fusion.1 = f32[2048,128]{1,0:T(8,128)S(1)} fusion(s32[16384]{0:T(1024)S(1)} %bitcast.57, f32[]{:T(128)} %constant.15.clone.1, bf16[4464,128]{1,0:T(8,128)(2,1)S(1)} %pad_maximum_fusion, s32[16384]{0:T(1024)S(1)} %broadcast_clamp_fusion.1), kind=kCustom, calls=%fused_computation.13 | custom fusion | flops 4194304 | bytes 2256900 | tf_op jit(solution)/shard_map/scatter-add | solution.py:58
  279.5 3.7 convert_reduce_fusion
  283.2 0.7 convolution_bitcast_fusion
  283.9 0.5 convolution_bitcast_fusion.1
  284.4 0.4 convolution_multiply_fusion
  285.1 136.6 %scatter_custom_fusion.3 = f32[4464,128]{1,0:T(8,128)} fusion(s32[16384]{0:T(1024)S(1)} %bitcast.55, f32[2048,128]{1,0:T(8,128)S(1)} %convolution_multiply_fusion, s32[16384]{0:T(1024)S(1)} %broadcast_clamp_fusion, f32[]{:T(128)} %constant.15.clone.1), kind=kCustom, calls=%fused_computation.11 | custom fusion | flops 2097152 | bytes 2285572 | tf_op jit(solution)/shard_map/scatter-add | solution.py:76
  421.7 1.3 fusion.8
  423.0 2.4 scatter_custom_fusion.4
  425.5 1.2 pad_maximum_fusion.1
  426.7 55.6 %all-to-all-start.1 = ((bf16[256,16,128]{2,1,0:T(8,128)(2,1)}), bf16[256,16,128]{2,1,0:T(8,128)(2,1)}, u32[]{:S(2)}, u32[]{:S(2)}) async-start(bf16[256,16,128]{2,1,0:T(8,128)(2,1)} %pad_maximum_fusion.1), calls=%async_computation.1 | async-start | bytes 2097152 | tf_op jit(solution)/shard_map/all_to_all | solution.py:86
  482.3 0.7 pad_maximum_fusion.2
  483.0 1.7 convolution_add_fusion.1
  484.7 269.6 %all-reduce.3.cloned.1.call-done = f32[65792]{0:T(1024)} async-done(((f32[65792]{0:T(1024)}), f32[65792]{0:T(1024)}) %all-reduce.3.cloned.1.call-update) | async-done | bytes 263184 | tf_op jit(solution)/shard_map/psum | solution.py:11
  754.3 1.0 fusion.21
  755.3 0.7 slice.58
  756.0 0.7 slice.56
  756.7 1.2 slice.76
  757.9 23.2 %scatter_custom_fusion.5 = f32[2048,128]{1,0:T(8,128)S(1)} fusion(f32[2048,128]{1,0:T(8,128)S(1)} %convolution_add_fusion.1, s32[4096]{0:T(1024)S(1)} %reshape.336, bf16[4096,128]{1,0:T(8,128)(2,1)} %bitcast.20), kind=kCustom, calls=%fused_computation.19 | custom fusion | flops 1048576 | bytes 2097152 | tf_op jit(solution)/shard_map/scatter-add | solution.py:89
  781.2 0.8 convert_element_type.32
  (46 shorter events, 1.5 us)
Async XLA Ops:
  7.2 272.4 %copy-start = (bf16[128,256]{1,0:T(8,128)(2,1)S(1)}, bf16[128,256]{1,0:T(8,128)(2,1)}, u32[]{:S(2)}) copy-start(bf16[128,256]{1,0:T(8,128)(2,1)} %param.12) | copy-start | bytes 196612
  7.2 10.6 %copy-start.6 = (s32[368]{0:T(512)S(1)}, s32[368]{0:T(512)}, u32[]{:S(2)}) copy-start(s32[368]{0:T(512)} %param.16) | copy-start | bytes 4420
  7.2 12.0 %copy-start.5 = (s32[1,256,8]{1,2,0:T(8,128)S(1)}, s32[1,256,8]{1,2,0:T(8,128)}, u32[]{:S(2)}) copy-start(s32[1,256,8]{1,2,0:T(8,128)} %param.15) | copy-start | bytes 24580
  7.2 12.3 %copy-start.1 = (bf16[2048,128]{1,0:T(8,128)(2,1)S(1)}, bf16[2048,128]{1,0:T(8,128)(2,1)}, u32[]{:S(2)}) copy-start(bf16[2048,128]{1,0:T(8,128)(2,1)} %param.10) | copy-start | bytes 1572868
  34.6 15.4 %copy-start.3 = (s32[1,16384]{1,0:T(1,128)S(1)}, s32[1,16384]{1,0:T(1,128)}, u32[]{:S(2)}) copy-start(s32[1,16384]{1,0:T(1,128)} %param.18) | copy-start | bytes 196612
  34.6 15.4 %copy-start.4 = (s32[1,16384]{1,0:T(1,128)S(1)}, s32[1,16384]{1,0:T(1,128)}, u32[]{:S(2)}) copy-start(s32[1,16384]{1,0:T(1,128)} %param.17) | copy-start | bytes 196612
  34.6 103.5 %copy-start.2 = (bf16[128,256]{1,0:T(8,128)(2,1)S(1)}, bf16[128,256]{1,0:T(8,128)(2,1)}, u32[]{:S(2)}) copy-start(bf16[128,256]{1,0:T(8,128)(2,1)} %param.11) | copy-start | bytes 196612
  34.6 105.3 %all-to-all-start = ((bf16[256,16,128]{2,1,0:T(8,128)(2,1)}), bf16[256,16,128]{2,1,0:T(8,128)(2,1)S(1)}, u32[]{:S(2)}, u32[]{:S(2)}) async-start(bf16[256,16,128]{2,1,0:T(8,128)(2,1)} %bitcast.8), calls=%async_computation | async-start | bytes 2097152 | tf_op jit(solution)/shard_map/all_to_all | solution.py:50
  141.4 138.2 %copy-start.7 = (f32[256]{0:T(256)S(1)}, f32[256]{0:T(256)}, u32[]{:S(2)}) copy-start(f32[256]{0:T(256)} %param.13) | copy-start | bytes 3076
  426.7 331.3 %all-to-all-start.1 = ((bf16[256,16,128]{2,1,0:T(8,128)(2,1)}), bf16[256,16,128]{2,1,0:T(8,128)(2,1)}, u32[]{:S(2)}, u32[]{:S(2)}) async-start(bf16[256,16,128]{2,1,0:T(8,128)(2,1)} %pad_maximum_fusion.1), calls=%async_computation.1 | async-start | bytes 2097152 | tf_op jit(solution)/shard_map/all_to_all | solution.py:86
  482.2 272.1 %all-reduce.3.cloned.1.call-start = ((), (), s32[]{:S(2)}) async-start(), calls=%async_computation.2 | async-start | bytes 532480 | tf_op jit(solution)/shard_map/psum | solution.py:11
Sparse Core Ops, SparseCore 0:
  489.2 265.1 all-reduce.2
where the time goes:
time: 789 us
  other arithmetic  397 us (50%)
  waiting for transfers between devices  270 us (34%)
  starting transfers between devices  70.3 us (9%)
  local copies, waits for them, and re-layouts  26.3 us (3%)
  between operations  17 us (2%)
  matrix products  8.73 us (1%)
    psum x1, waiting for transfers between devices, together(): total = lax.psum(line, axis)  270 us
    scatter-add x1, other arithmetic, body(): jax.ops.segment_sum(source_table[edge_from].astype(jnp.float32), drop_to,...  138 us
    scatter-add x1, other arithmetic, body(): jax.ops.segment_sum(spread[edge_to], drop_from, num_segments=table_rows)  137 us
    scatter-add x1, other arithmetic, body(): jax.ops.segment_sum(is_real.astype(jnp.float32), drop_to, num_segments=lo...  87.5 us
    all_to_all x1, starting transfers between devices, body(): lax.all_to_all(outgoing.astype(jnp.bfloat16), 'vert', split_axis=0, conca...  55.6 us
    scatter-add x1, other arithmetic, body(): jax.ops.segment_sum(returned.reshape(-1, feat_width), sent_rows.reshape(-...  23.2 us
  transfers between devices with their start and end apart: 3, of which 1 were waited for; matrix products, arithmetic and copies ran while one was open for 12% of the time, Pallas kernels for 0%

commit v1 on v0

v1 whole, which is shorter than its diff:
```python
import functools

import jax
import jax.numpy as jnp
from jax import lax
from jax.experimental import pallas as pl
from jax.experimental.pallas import tpu as pltpu
from jax.sharding import PartitionSpec as P

HUB_MOST = 8
STREAMS = 8
UNROLL = 4
GROUP = STREAMS * UNROLL
LIMIT = 60 * 1024 * 1024
F32 = jnp.float32
BF16 = jnp.bfloat16
SMEM = pl.BlockSpec(memory_space=pltpu.SMEM)
VMEM = pl.BlockSpec(memory_space=pltpu.VMEM)


def up(n, k):
    return -(-n // k) * k


def row(i):
    return pl.ds(i, 1)


def clear(refs, rows, step):
    def some(i, _):
        at = pl.ds(pl.multiple_of(i * step, step), step)
        for ref in refs:
            ref[at, :] = jnp.zeros((step, ref.shape[1]), F32)
        return 0

    lax.fori_loop(0, rows // step, some, 0)


def add_rows(trips, take, put, table, sums):
    def some(i, _):
        for j in range(GROUP):
            e = i * GROUP + j
            to = row(put[e])
            ref = sums[j % STREAMS]
            ref[to, :] = ref[to, :] + table[row(take[e]), :]
        return 0

    lax.fori_loop(0, trips, some, 0)


def total(sums, at):
    parts = [ref[at, :] for ref in sums]
    while len(parts) > 1:
        parts = [a + b for a, b in zip(parts[::2], parts[1::2])]
    return parts[0]


def widen(ref, table, slots, first, start):
    blocks = 16

    def some(i, _):
        part = ref[pl.ds(i * blocks, blocks), first : first + slots, :]
        at = pl.multiple_of(start + i * blocks * slots, 8)
        table[pl.ds(at, blocks * slots), :] = part.astype(F32).reshape(blocks * slots, -1)
        return 0

    lax.fori_loop(0, ref.shape[0] // blocks, some, 0)


def gather_kernel(send_ref, hub_ref, feats_ref, out_ref, table, rows):
    peers, depth, width = out_ref.shape
    slots = depth - HUB_MOST
    table[...] = feats_ref[...].astype(F32)

    def some(i, _):
        for j in range(GROUP):
            e = i * GROUP + j
            rows[row(e), :] = table[row(send_ref[e]), :]
        return 0

    lax.fori_loop(0, peers * slots // GROUP, some, 0)
    hubs = jnp.concatenate([table[row(hub_ref[j]), :] for j in range(HUB_MOST)], axis=0)
    hubs = jnp.broadcast_to(hubs[None], (16, HUB_MOST, width)).astype(BF16)

    def pack(i, _):
        at = pl.multiple_of(i * 16 * slots, 8)
        own = rows[pl.ds(at, 16 * slots), :].reshape(16, slots, width).astype(BF16)
        out_ref[pl.ds(i * 16, 16), :slots, :] = own
        out_ref[pl.ds(i * 16, 16), slots:, :] = hubs
        return 0

    lax.fori_loop(0, peers // 16, pack, 0)


def layer_kernel(
    trips_ref, src_ref, dst_ref, place_ref,
    feats_ref, arrived_ref, inverse_ref, cot_ref, w_self_ref, w_neigh_ref, bias_ref,
    out_ref, own_ref, outgoing_ref, grads_ref,
    table, hub_slots, spread, *sums,
):
    local, width = feats_ref.shape
    peers, depth, _ = arrived_ref.shape
    slots = depth - HUB_MOST
    hubs = place_ref.shape[0]
    wide = w_self_ref.shape[1]
    halo_end = local + peers * slots
    trips = trips_ref[0]
    step = 256

    clear(sums, up(local + 1, 64), 64)
    table[:local, :] = feats_ref[...].astype(F32)
    widen(arrived_ref, table, slots, 0, local)
    widen(arrived_ref, hub_slots, HUB_MOST, slots, 0)

    def hub_in(i, _):
        for j in range(8):
            h = i * 8 + j
            table[row(halo_end + h), :] = hub_slots[row(place_ref[h]), :]
        return 0

    lax.fori_loop(0, hubs // 8, hub_in, 0)
    add_rows(trips, src_ref, dst_ref, table, sums)

    grads_ref[...] = jnp.zeros_like(grads_ref)
    w_self, w_neigh, bias = w_self_ref[...], w_neigh_ref[...], bias_ref[...]
    outer = (((0,), (0,)), ((), ()))
    back = (((1,), (1,)), ((), ()))

    def dense(i, _):
        at = pl.ds(pl.multiple_of(i * step, step), step)
        feats = feats_ref[at, :]
        inverse = inverse_ref[at, :]
        mean = (total(sums, at) * inverse).astype(BF16)
        linear = jnp.dot(feats, w_self, preferred_element_type=F32)
        linear = linear + jnp.dot(mean, w_neigh, preferred_element_type=F32) + bias
        logistic = jax.nn.sigmoid(linear)
        out_ref[at, :] = (linear * logistic).astype(BF16)
        slope = logistic * (1.0 + linear * (1.0 - logistic))
        grad = (cot_ref[at, :].astype(F32) * slope).astype(BF16)
        grads_ref[:width, :] += lax.dot_general(feats, grad, outer, preferred_element_type=F32)
        grads_ref[width : 2 * width, :] += lax.dot_general(
            mean, grad, outer, preferred_element_type=F32
        )
        grads_ref[2 * width : 2 * width + 8, :] += jnp.sum(
            grad.astype(F32).reshape(step // 8, 8, wide), axis=0
        )
        own_ref[at, :] = lax.dot_general(grad, w_self, back, preferred_element_type=F32)
        spread[at, :] = lax.dot_general(grad, w_neigh, back, preferred_element_type=F32) * inverse
        return 0

    lax.fori_loop(0, local // step, dense, 0)

    clear(sums, sums[0].shape[0], 64)
    spread[local : local + 8, :] = jnp.zeros((8, width), F32)
    add_rows(trips, dst_ref, src_ref, spread, sums)

    def own_part(i, _):
        at = pl.ds(pl.multiple_of(i * step, step), step)
        own_ref[at, :] += total(sums, at)
        return 0

    lax.fori_loop(0, local // step, own_part, 0)

    def halo_part(i, _):
        at = pl.ds(pl.multiple_of(local + i * 16 * slots, 8), 16 * slots)
        part = total(sums, at).reshape(16, slots, width).astype(BF16)
        outgoing_ref[pl.ds(i * 16, 16), :slots, :] = part
        return 0

    lax.fori_loop(0, peers // 16, halo_part, 0)

    clear((hub_slots,), peers * HUB_MOST, 64)

    def hub_part(i, _):
        at = pl.ds(pl.multiple_of(halo_end + i * 8, 8), 8)
        table[pl.ds(pl.multiple_of(i * 8, 8), 8), :] = total(sums, at)
        return 0

    lax.fori_loop(0, hubs // 8, hub_part, 0)

    def hub_out(i, _):
        for j in range(8):
            h = i * 8 + j
            hub_slots[row(place_ref[h]), :] = table[row(h), :]
        return 0

    lax.fori_loop(0, hubs // 8, hub_out, 0)

    def hub_pack(i, _):
        at = pl.ds(pl.multiple_of(i * 16 * HUB_MOST, 8), 16 * HUB_MOST)
        part = hub_slots[at, :].reshape(16, HUB_MOST, width).astype(BF16)
        outgoing_ref[pl.ds(i * 16, 16), slots:, :] = part
        return 0

    lax.fori_loop(0, peers // 16, hub_pack, 0)


def final_kernel(send_ref, hub_ref, own_ref, returned_ref, out_ref, rows, hub_sum, *sums):
    peers, depth, width = returned_ref.shape
    slots = depth - HUB_MOST
    local = own_ref.shape[0]
    step = 256
    sums[0][:local, :] = own_ref[...]
    clear(sums[1:], up(local + 1, 8) // 8 * 8, 8)
    widen(returned_ref, rows, slots, 0, 0)

    def some(i, _):
        for j in range(GROUP):
            e = i * GROUP + j
            to = row(send_ref[e])
            ref = sums[j % STREAMS]
            ref[to, :] = ref[to, :] + rows[row(e), :]
        return 0

    lax.fori_loop(0, peers * slots // GROUP, some, 0)

    def hub_add(i, acc):
        part = returned_ref[pl.ds(i * 16, 16), slots:, :].astype(F32)
        return acc + jnp.sum(part, axis=0)

    hub_sum[...] = lax.fori_loop(0, peers // 16, hub_add, jnp.zeros((HUB_MOST, width), F32))
    for j in range(HUB_MOST):
        to = row(hub_ref[j])
        sums[0][to, :] = sums[0][to, :] + hub_sum[row(j), :]

    def close(i, _):
        at = pl.ds(pl.multiple_of(i * step, step), step)
        out_ref[at, :] = total(sums, at).astype(BF16)
        return 0

    lax.fori_loop(0, local // step, close, 0)


def body(
    feats, w_self, w_neigh, bias, cotangent, send_rows, hub_ids, edge_src, edge_dst, edge_count
):
    local, width = feats.shape
    wide = w_self.shape[1]
    peers = lax.axis_size("vert")
    me = lax.axis_index("vert")
    slots = send_rows.shape[2]
    depth = slots + HUB_MOST
    hub_total = hub_ids.shape[0]
    table_rows = local + peers * slots + hub_total
    edge_total = edge_src.shape[1]
    params = pltpu.CompilerParams(vmem_limit_bytes=LIMIT)

    send = send_rows.reshape(-1)
    hub_owner = hub_ids // local
    hub_local = hub_ids - hub_owner * local
    order = lax.iota(jnp.int32, hub_total)
    first = jnp.sum((hub_owner < me).astype(jnp.int32))
    picked = (hub_owner == me)[None, :] & (
        (order - first)[None, :] == lax.iota(jnp.int32, HUB_MOST)[:, None]
    )
    own_count = jnp.sum((hub_owner == me).astype(jnp.int32))
    own_hubs = jnp.sum(jnp.where(picked, hub_local[None, :], 0), axis=1)
    own_back = jnp.where(lax.iota(jnp.int32, HUB_MOST) < own_count, own_hubs, local)
    before = jnp.sum((hub_owner[None, :] < hub_owner[:, None]).astype(jnp.int32), axis=1)
    place = hub_owner * HUB_MOST + order - before

    sent = pl.pallas_call(
        gather_kernel,
        out_shape=jax.ShapeDtypeStruct((peers, depth, width), BF16),
        in_specs=[SMEM, SMEM, VMEM],
        out_specs=VMEM,
        scratch_shapes=[
            pltpu.VMEM((local, width), F32),
            pltpu.VMEM((peers * slots, width), F32),
        ],
        compiler_params=params,
        name="gather_sent",
    )(send, own_hubs, feats)
    arrived = lax.all_to_all(sent, "vert", split_axis=0, concat_axis=0, tiled=True)

    is_real = lax.iota(jnp.int32, edge_total) < edge_count[0]
    dst = jnp.where(is_real, edge_dst[0], local)
    src = jnp.where(is_real, edge_src[0], table_rows)
    trips = (edge_count + (GROUP - 1)) // GROUP
    lanes = 128
    high = (dst // lanes)[:, None] == lax.iota(jnp.int32, local // lanes)[None, :]
    low = (dst % lanes)[:, None] == lax.iota(jnp.int32, lanes)[None, :]
    degree = lax.dot_general(
        high.astype(BF16), low.astype(BF16), (((0,), (0,)), ((), ())), preferred_element_type=F32
    ).reshape(-1)
    inverse = jnp.broadcast_to((1.0 / jnp.maximum(degree, 1.0))[:, None], (local, width))

    rows_up = up(table_rows + 1, 64)
    output, own, outgoing, grads = pl.pallas_call(
        layer_kernel,
        out_shape=(
            jax.ShapeDtypeStruct((local, wide), BF16),
            jax.ShapeDtypeStruct((local, width), F32),
            jax.ShapeDtypeStruct((peers, depth, width), BF16),
            jax.ShapeDtypeStruct((2 * width + 8, wide), F32),
        ),
        in_specs=[SMEM] * 4 + [VMEM] * 7,
        out_specs=(VMEM,) * 4,
        scratch_shapes=[
            pltpu.VMEM((rows_up, width), F32),
            pltpu.VMEM((peers * HUB_MOST, width), F32),
            pltpu.VMEM((up(local + 1, 8), width), F32),
        ]
        + [pltpu.VMEM((rows_up, width), F32)] * STREAMS,
        compiler_params=params,
        name="layer",
    )(trips, src, dst, place, feats, arrived, inverse, cotangent, w_self, w_neigh, bias[None, :])

    summed = lax.psum(grads, "vert")
    returned = lax.all_to_all(outgoing, "vert", split_axis=0, concat_axis=0, tiled=True)
    grad_feats = pl.pallas_call(
        final_kernel,
        out_shape=jax.ShapeDtypeStruct((local, width), BF16),
        in_specs=[SMEM, SMEM, VMEM, VMEM],
        out_specs=VMEM,
        scratch_shapes=[
            pltpu.VMEM((peers * slots, width), F32),
            pltpu.VMEM((HUB_MOST, width), F32),
        ]
        + [pltpu.VMEM((up(local + 1, 8), width), F32)] * STREAMS,
        compiler_params=params,
        name="final",
    )(send, own_back, own, returned)
    grad_bias = jnp.sum(summed[2 * width :], axis=0)
    return (output, grad_feats, summed[:width], summed[width : 2 * width], grad_bias)


def solution(mesh):
    in_specs = (
        P("vert", None),
        P(),
        P(),
        P(),
        P("vert", None),
        P("vert", None, None),
        P(),
        P("vert", None),
        P("vert", None),
        P("vert"),
    )
    out_specs = (P("vert", None), P("vert", None), P(), P(), P())
    return jax.shard_map(body, mesh=mesh, in_specs=in_specs, out_specs=out_specs, check_vma=False)
```

time: 789 us -> 424 us (0.54)
  other arithmetic: 397 us -> 7.85 us
  Pallas kernels: 0 us -> 73.8 us
  starting transfers between devices: 70.3 us -> 20.8 us
  waiting for transfers between devices: 270 us -> 298 us
  local copies, waits for them, and re-layouts: 26.3 us -> 5.58 us
    scatter-add x6 -> x0, other arithmetic: 392 us -> none  [the longest x1 138 us: body(): jax.ops.segment_sum(source_table[edge_from].astype(jnp.float32), drop_to,...]
    pallas_call x0 -> x3, Pallas kernels: none -> 73.8 us  [the longest x1 62.2 us: body(): pl.pallas_call(layer_kernel, out_shape=(jax.ShapeDtypeStruct((local, wide...]
    all_to_all x2, starting transfers between devices: 70.3 us -> 20.8 us  [the longest x1 14.7 us: body(): lax.all_to_all(sent, 'vert', split_axis=0, concat_axis=0, tiled=True)]
    all_to_all x2, waiting for transfers between devices: 0.01 us -> 27.2 us  [the longest x1 27.2 us: body(): lax.all_to_all(sent, 'vert', split_axis=0, concat_axis=0, tiled=True)]
    gather x3 -> x0, local copies, waits for them, and re-layouts: 19.3 us -> none  [the longest x1 15 us: body(): feats[sent_rows]]
  transfers between devices with their start and end apart: 3 -> 3, of which waited for: 1 -> 2; matrix products, arithmetic and copies ran while one was open for 12% -> 2% of each run, Pallas kernels for 0% -> 0%
where the time goes in v1:
time: 424 us; the launch traced here: 423 us
  waiting for transfers between devices  298 us (70%)
  Pallas kernels  73.8 us (17%)
  starting transfers between devices  20.8 us (5%)
  between operations  14.8 us (3%)
  other arithmetic  7.85 us (2%)
  local copies, waits for them, and re-layouts  5.58 us (1%)
    psum x1, waiting for transfers between devices, body(): summed = lax.psum(grads, 'vert')  270 us
    pallas_call x1, Pallas kernels, body(): pl.pallas_call(layer_kernel, out_shape=(jax.ShapeDtypeStruct((local, wide...  62.2 us
    all_to_all x1, waiting for transfers between devices, body(): lax.all_to_all(sent, 'vert', split_axis=0, concat_axis=0, tiled=True)  27.2 us
    all_to_all x1, starting transfers between devices, body(): lax.all_to_all(sent, 'vert', split_axis=0, concat_axis=0, tiled=True)  14.7 us
  transfers between devices with their start and end apart: 3, of which 2 were waited for; matrix products, arithmetic and copies ran while one was open for 2% of the time, Pallas kernels for 0%

profile of v1, /device:TPU:2, one launch (start us, length us, event | category | flops | bytes accessed | tf_op | source)
XLA Modules:
  0.0 423.3 jit_solution(5099574246050181873)
XLA Ops:
  7.2 1.3 convert_reduce_fusion.1
  8.5 0.2 convert_reduce_fusion
  8.7 1.9 convert_reduce_fusion.2
  10.6 0.6 iota_subtract_fusion
  11.3 0.8 copy.16
  12.1 0.7 reshape.76.send_ref
  12.8 0.6 select_reduce_fusion.hub_ref
  13.4 4.2 gather_sent.1
  17.6 0.0 copy-start.3
  17.6 0.0 copy-start.4
  17.6 14.7 %all-to-all-start = ((bf16[256,16,128]{2,1,0:T(8,128)(2,1)}), bf16[256,16,128]{2,1,0:T(8,128)(2,1)S(1)}, u32[]{:S(2)}, u32[]{:S(2)}) async-start(bf16[256,16,128]{2,1,0:T(8,128)(2,1)} %gather_sent.1), calls=%async_computation | async-start | bytes 2097152 | tf_op jit(solution)/shard_map/all_to_all | solution.py:274
  33.0 0.0 copy-done.3
  33.0 0.0 copy-done.4
  33.0 0.7 add_select_fusion.1
  33.7 0.0 copy-start.2
  33.7 2.3 fusion.4
  36.1 0.0 copy-done.2
  36.1 27.2 %all-to-all-done.arrived_ref = bf16[256,16,128]{2,1,0:T(8,128)(2,1)S(1)} async-done(((bf16[256,16,128]{2,1,0:T(8,128)(2,1)}), bf16[256,16,128]{2,1,0:T(8,128)(2,1)S(1)}, u32[]{:S(2)}, u32[]{:S(2)}) %all-to-all-start) | async-done | bytes 1048608 | tf_op jit(solution)/shard_map/all_to_all | solution.py:274
  63.2 1.3 broadcast_in_dim.46.inverse_ref
  64.6 0.0 copy-done.1
  64.6 62.2 %layer.1 = (bf16[2048,256]{1,0:T(8,128)(2,1)}, f32[2048,128]{1,0:T(8,128)}, bf16[256,16,128]{2,1,0:T(8,128)(2,1)}, f32[264,256]{1,0:T(8,128)}) custom-call(s32[1]{0:T(128)S(6)} %select_n.45.trips_ref, s32[16384]{0:T(1024)} %get-tuple-element.23.src_ref, s32[16384]{0:T(1024)} %copy-done.2, s32[368]{0:T(512)} %get-tuple-element.22.place_ref, ...), custom_call_target="tpu_custom_call" | custom-call | tf_op jit(solution)/shard_map/layer/pallas_call | solution.py:289
  126.8 6.1 %all-to-all-start.1 = ((bf16[256,16,128]{2,1,0:T(8,128)(2,1)}), bf16[256,16,128]{2,1,0:T(8,128)(2,1)S(1)}, u32[]{:S(2)}, u32[]{:S(2)}) async-start(bf16[256,16,128]{2,1,0:T(8,128)(2,1)} %get-tuple-element.11), calls=%async_computation.1 | async-start | bytes 2097152 | tf_op jit(solution)/shard_map/all_to_all | solution.py:310
  132.9 0.0 all-reduce.2.cloned.1.call-start
  132.9 0.7 all-reduce.2.cloned.1.call-update
  133.6 0.0 copy-done.5
  133.6 1.2 compare_select_fusion.hub_ref
  134.8 270.3 %all-reduce.2.cloned.1.call-done = f32[264,256]{1,0:T(8,128)} async-done(((f32[264,256]{1,0:T(8,128)}), f32[264,256]{1,0:T(8,128)}) %all-reduce.2.cloned.1.call-update) | async-done | bytes 270352 | tf_op jit(solution)/shard_map/psum | solution.py:309
  405.1 1.3 slice_reduce_fusion
  406.4 1.7 fusion.14
  408.0 0.0 all-to-all-done.1.returned_ref
  408.0 1.0 copy-done
  409.1 7.4 %final.1 = bf16[2048,128]{1,0:T(8,128)(2,1)} custom-call(s32[2048]{0:T(1024)} %reshape.76.send_ref, s32[8]{0:T(128)} %compare_select_fusion.hub_ref, f32[2048,128]{1,0:T(8,128)} %get-tuple-element.10.own_ref, bf16[256,16,128]{2,1,0:T(8,128)(2,1)} %copy-done), custom_call_target="tpu_custom_call" | custom-call | tf_op jit(solution)/shard_map/final/pallas_call | solution.py:311
  (4 shorter events, 0.0 us)
Async XLA Ops:
  17.6 15.4 %copy-start.3 = (s32[1,16384]{1,0:T(1,128)S(1)}, s32[1,16384]{1,0:T(1,128)}, u32[]{:S(2)}) copy-start(s32[1,16384]{1,0:T(1,128)} %param.18) | copy-start | bytes 196612
  17.6 15.4 %copy-start.4 = (s32[1,16384]{1,0:T(1,128)S(1)}, s32[1,16384]{1,0:T(1,128)}, u32[]{:S(2)}) copy-start(s32[1,16384]{1,0:T(1,128)} %param.17) | copy-start | bytes 196612
  17.6 45.6 %all-to-all-start = ((bf16[256,16,128]{2,1,0:T(8,128)(2,1)}), bf16[256,16,128]{2,1,0:T(8,128)(2,1)S(1)}, u32[]{:S(2)}, u32[]{:S(2)}) async-start(bf16[256,16,128]{2,1,0:T(8,128)(2,1)} %gather_sent.1), calls=%async_computation | async-start | bytes 2097152 | tf_op jit(solution)/shard_map/all_to_all | solution.py:274
  33.7 2.4 copy-start.2
  63.2 1.3 copy-start.1
  126.8 6.8 %copy-start.5 = (s32[8]{0:T(128)S(1)}, s32[8]{0:T(128)}, u32[]{:S(2)}) copy-start(s32[8]{0:T(128)} %select_reduce_fusion.hub_ref) | copy-start | bytes 100
  126.8 281.2 %all-to-all-start.1 = ((bf16[256,16,128]{2,1,0:T(8,128)(2,1)}), bf16[256,16,128]{2,1,0:T(8,128)(2,1)S(1)}, u32[]{:S(2)}, u32[]{:S(2)}) async-start(bf16[256,16,128]{2,1,0:T(8,128)(2,1)} %get-tuple-element.11), calls=%async_computation.1 | async-start | bytes 2097152 | tf_op jit(solution)/shard_map/all_to_all | solution.py:310
  132.9 272.2 %all-reduce.2.cloned.1.call-start = ((), (), s32[]{:S(2)}) async-start(), calls=%async_computation.2 | async-start | bytes 540672 | tf_op jit(solution)/shard_map/psum | solution.py:309
  408.0 1.0 copy-start
Sparse Core Ops, SparseCore 0:
  139.8 265.2 all-reduce.1

commit v2 on v1

--- a/solution.py
+++ b/solution.py
@@ -55,11 +55,11 @@
     return parts[0]
 
 
-def widen(ref, table, slots, first, start):
-    blocks = 16
+def widen(ref, table, start):
+    blocks, slots = 16, ref.shape[1]
 
     def some(i, _):
-        part = ref[pl.ds(i * blocks, blocks), first : first + slots, :]
+        part = ref[pl.ds(i * blocks, blocks)]
         at = pl.multiple_of(start + i * blocks * slots, 8)
         table[pl.ds(at, blocks * slots), :] = part.astype(F32).reshape(blocks * slots, -1)
         return 0
@@ -67,9 +67,8 @@
     lax.fori_loop(0, ref.shape[0] // blocks, some, 0)
 
 
-def gather_kernel(send_ref, hub_ref, feats_ref, out_ref, table, rows):
-    peers, depth, width = out_ref.shape
-    slots = depth - HUB_MOST
+def gather_kernel(send_ref, hub_ref, feats_ref, out_ref, hub_out_ref, table, rows):
+    peers, slots, width = out_ref.shape
     table[...] = feats_ref[...].astype(F32)
 
     def some(i, _):
@@ -80,13 +79,12 @@
 
     lax.fori_loop(0, peers * slots // GROUP, some, 0)
     hubs = jnp.concatenate([table[row(hub_ref[j]), :] for j in range(HUB_MOST)], axis=0)
-    hubs = jnp.broadcast_to(hubs[None], (16, HUB_MOST, width)).astype(BF16)
+    hub_out_ref[...] = hubs.astype(BF16)
 
     def pack(i, _):
         at = pl.multiple_of(i * 16 * slots, 8)
         own = rows[pl.ds(at, 16 * slots), :].reshape(16, slots, width).astype(BF16)
-        out_ref[pl.ds(i * 16, 16), :slots, :] = own
-        out_ref[pl.ds(i * 16, 16), slots:, :] = hubs
+        out_ref[pl.ds(i * 16, 16)] = own
         return 0
 
     lax.fori_loop(0, peers // 16, pack, 0)
@@ -94,13 +92,12 @@
 
 def layer_kernel(
     trips_ref, src_ref, dst_ref, place_ref,
-    feats_ref, arrived_ref, inverse_ref, cot_ref, w_self_ref, w_neigh_ref, bias_ref,
-    out_ref, own_ref, outgoing_ref, grads_ref,
+    feats_ref, halo_ref, hubs_ref, inverse_ref, cot_ref, w_self_ref, w_neigh_ref, bias_ref,
+    out_ref, own_ref, halo_back_ref, hub_back_ref, grads_ref,
     table, hub_slots, spread, *sums,
 ):
     local, width = feats_ref.shape
-    peers, depth, _ = arrived_ref.shape
-    slots = depth - HUB_MOST
+    peers, slots, _ = halo_ref.shape
     hubs = place_ref.shape[0]
     wide = w_self_ref.shape[1]
     halo_end = local + peers * slots
@@ -109,8 +106,8 @@
 
     clear(sums, up(local + 1, 64), 64)
     table[:local, :] = feats_ref[...].astype(F32)
-    widen(arrived_ref, table, slots, 0, local)
-    widen(arrived_ref, hub_slots, HUB_MOST, slots, 0)
+    widen(halo_ref, table, local)
+    widen(hubs_ref, hub_slots, 0)
 
     def hub_in(i, _):
         for j in range(8):
@@ -137,13 +134,13 @@
         out_ref[at, :] = (linear * logistic).astype(BF16)
         slope = logistic * (1.0 + linear * (1.0 - logistic))
         grad = (cot_ref[at, :].astype(F32) * slope).astype(BF16)
-        grads_ref[:width, :] += lax.dot_general(feats, grad, outer, preferred_element_type=F32)
-        grads_ref[width : 2 * width, :] += lax.dot_general(
+        grads_ref[:width, :wide] += lax.dot_general(feats, grad, outer, preferred_element_type=F32)
+        grads_ref[width : 2 * width, :wide] += lax.dot_general(
             mean, grad, outer, preferred_element_type=F32
         )
-        grads_ref[2 * width : 2 * width + 8, :] += jnp.sum(
-            grad.astype(F32).reshape(step // 8, 8, wide), axis=0
-        )
+        grad_sum = jnp.sum(grad.astype(F32).reshape(step // 8, 8, wide), axis=0)
+        for j in range(wide // width):
+            grads_ref[8 * j : 8 * j + 8, wide:] += grad_sum[:, j * width : (j + 1) * width]
         own_ref[at, :] = lax.dot_general(grad, w_self, back, preferred_element_type=F32)
         spread[at, :] = lax.dot_general(grad, w_neigh, back, preferred_element_type=F32) * inverse
         return 0
@@ -164,7 +161,7 @@
     def halo_part(i, _):
         at = pl.ds(pl.multiple_of(local + i * 16 * slots, 8), 16 * slots)
         part = total(sums, at).reshape(16, slots, width).astype(BF16)
-        outgoing_ref[pl.ds(i * 16, 16), :slots, :] = part
+        halo_back_ref[pl.ds(i * 16, 16)] = part
         return 0
 
     lax.fori_loop(0, peers // 16, halo_part, 0)
@@ -189,20 +186,19 @@
     def hub_pack(i, _):
         at = pl.ds(pl.multiple_of(i * 16 * HUB_MOST, 8), 16 * HUB_MOST)
         part = hub_slots[at, :].reshape(16, HUB_MOST, width).astype(BF16)
-        outgoing_ref[pl.ds(i * 16, 16), slots:, :] = part
+        hub_back_ref[pl.ds(i * 16, 16)] = part
         return 0
 
     lax.fori_loop(0, peers // 16, hub_pack, 0)
 
 
-def final_kernel(send_ref, hub_ref, own_ref, returned_ref, out_ref, rows, hub_sum, *sums):
-    peers, depth, width = returned_ref.shape
-    slots = depth - HUB_MOST
+def final_kernel(send_ref, hub_ref, own_ref, returned_ref, hub_sum, out_ref, rows, *sums):
+    peers, slots, width = returned_ref.shape
     local = own_ref.shape[0]
     step = 256
     sums[0][:local, :] = own_ref[...]
-    clear(sums[1:], up(local + 1, 8) // 8 * 8, 8)
-    widen(returned_ref, rows, slots, 0, 0)
+    clear(sums[1:], up(local + 1, 8), 8)
+    widen(returned_ref, rows, 0)
 
     def some(i, _):
         for j in range(GROUP):
@@ -214,11 +210,6 @@
 
     lax.fori_loop(0, peers * slots // GROUP, some, 0)
 
-    def hub_add(i, acc):
-        part = returned_ref[pl.ds(i * 16, 16), slots:, :].astype(F32)
-        return acc + jnp.sum(part, axis=0)
-
-    hub_sum[...] = lax.fori_loop(0, peers // 16, hub_add, jnp.zeros((HUB_MOST, width), F32))
     for j in range(HUB_MOST):
         to = row(hub_ref[j])
         sums[0][to, :] = sums[0][to, :] + hub_sum[row(j), :]
@@ -229,6 +220,178 @@
         return 0
 
     lax.fori_loop(0, local // step, close, 0)
+
+
+PLANE = 32
+MESH = pl.DeviceIdType.MESH
+
+
+class Places:
+    def __init__(self):
+        self.count = lax.axis_size("vert")
+        self.planes = self.count // PLANE
+        self.me = lax.axis_index("vert")
+        self.z = lax.div(self.me, PLANE)
+        self.p = lax.rem(self.me, PLANE)
+
+    def in_plane(self, i):
+        p = lax.rem(self.p + i, PLANE)
+        return p, self.z * PLANE + p
+
+    def in_line(self, i):
+        z = lax.rem(self.z + i, self.planes)
+        return z, z * PLANE + self.p
+
+    def barrier(self, ready):
+        entry = pltpu.get_barrier_semaphore()
+
+        def greet_plane(i, _):
+            pl.semaphore_signal(entry, device_id=(self.in_plane(i)[1],), device_id_type=MESH)
+            return 0
+
+        def greet_line(i, _):
+            pl.semaphore_signal(entry, device_id=(self.in_line(i)[1],), device_id_type=MESH)
+            return 0
+
+        def vouch(i, _):
+            pl.semaphore_signal(ready, device_id=(self.in_line(i)[1],), device_id_type=MESH)
+            return 0
+
+        lax.fori_loop(1, PLANE, greet_plane, 0)
+        lax.fori_loop(1, self.planes, greet_line, 0)
+        pl.semaphore_wait(entry, PLANE + self.planes - 2)
+        lax.fori_loop(1, self.planes, vouch, 0)
+        pl.semaphore_wait(ready, self.planes - 1)
+
+    def copy(self, src, dst, sems, to):
+        return pltpu.make_async_remote_copy(
+            src_ref=src,
+            dst_ref=dst,
+            send_sem=sems.at[0],
+            recv_sem=sems.at[1],
+            device_id=(to,),
+            device_id_type=MESH,
+        )
+
+    def all_of(self, ref, sems):
+        return self.copy(ref, ref, sems, lax.rem(self.me + 1, self.count))
+
+    def send_blocks(self, src, dst, sems, start, stop):
+        def some(k, _):
+            t = lax.rem(self.me * 75 + k * 159, self.count)
+
+            @pl.when(t != self.me)
+            def _():
+                self.copy(src.at[t], dst.at[self.me], sems, t).start()
+
+            return 0
+
+        lax.fori_loop(start, stop, some, 0)
+
+
+def forward_kernel(sent_ref, hub_ref, halo_ref, hubs_ref, a, b, c, keep, ready):
+    here = Places()
+    here.barrier(ready)
+    own_hub = pltpu.make_async_copy(hub_ref, hubs_ref.at[here.p, here.z], keep.at[0])
+    own_hub.start()
+    own_halo = pltpu.make_async_copy(sent_ref.at[here.me], halo_ref.at[here.me], keep.at[1])
+    own_halo.start()
+
+    def along(i, _):
+        here.copy(hub_ref, hubs_ref.at[here.p, here.z], a, here.in_line(i)[1]).start()
+        return 0
+
+    lax.fori_loop(1, here.planes, along, 0)
+    here.send_blocks(sent_ref, halo_ref, b, 0, here.count // 2)
+    own_hub.wait()
+    here.all_of(hubs_ref.at[here.p, pl.ds(0, here.planes - 1)], a).wait()
+
+    def across(i, _):
+        here.copy(hubs_ref.at[here.p], hubs_ref.at[here.p], c, here.in_plane(i)[1]).start()
+        return 0
+
+    lax.fori_loop(1, PLANE, across, 0)
+    here.send_blocks(sent_ref, halo_ref, b, here.count // 2, here.count)
+    own_halo.wait()
+    here.all_of(hubs_ref.at[pl.ds(0, PLANE - 1)], c).wait()
+    here.all_of(halo_ref.at[pl.ds(0, here.count - 1)], b).wait()
+
+
+def backward_kernel(
+    back_ref, hub_ref, grads_ref, halo_ref, hub_sum_ref, whole_ref,
+    part_in, hub_in, grads_in, hub_part, hub_line, grad_part, grad_line,
+    a, b, c, d, e, f, keep, ready,
+):
+    here = Places()
+    part_in[...] = grads_ref[...].astype(BF16)
+    here.barrier(ready)
+    kept = [
+        pltpu.make_async_copy(back_ref.at[here.me], halo_ref.at[here.me], keep.at[0]),
+        pltpu.make_async_copy(hub_ref.at[here.p], hub_in.at[here.p], keep.at[1]),
+        pltpu.make_async_copy(part_in.at[here.p], grads_in.at[here.p], keep.at[2]),
+    ]
+    for copy in kept:
+        copy.start()
+
+    def across(i, _):
+        p, to = here.in_plane(i)
+        here.copy(part_in.at[p], grads_in.at[here.p], a, to).start()
+        here.copy(hub_ref.at[p], hub_in.at[here.p], b, to).start()
+        return 0
+
+    lax.fori_loop(1, PLANE, across, 0)
+    third = here.count // 3
+    here.send_blocks(back_ref, halo_ref, c, 0, third)
+    for copy in kept:
+        copy.wait()
+    here.all_of(grads_in.at[pl.ds(0, PLANE - 1)], a).wait()
+    here.all_of(hub_in.at[pl.ds(0, PLANE - 1)], b).wait()
+    grad_part[...] = lax.fori_loop(
+        0, PLANE, lambda i, acc: acc + grads_in[i].astype(F32), jnp.zeros(grad_part.shape, F32)
+    )
+    hub_part[...] = lax.fori_loop(
+        0, PLANE, lambda i, acc: acc + hub_in[i].astype(F32), jnp.zeros(hub_part.shape, F32)
+    )
+    here.send_blocks(back_ref, halo_ref, c, third, third + 8)
+    kept = [
+        pltpu.make_async_copy(grad_part, grad_line.at[here.z], keep.at[0]),
+        pltpu.make_async_copy(hub_part.at[here.z], hub_line.at[here.z], keep.at[1]),
+    ]
+    for copy in kept:
+        copy.start()
+
+    def along(i, _):
+        z, to = here.in_line(i)
+        here.copy(grad_part, grad_line.at[here.z], d, to).start()
+        here.copy(hub_part.at[z], hub_line.at[here.z], e, to).start()
+        return 0
+
+    lax.fori_loop(1, here.planes, along, 0)
+    here.send_blocks(back_ref, halo_ref, c, third + 8, 2 * third)
+    for copy in kept:
+        copy.wait()
+    here.all_of(grad_line.at[pl.ds(0, here.planes - 1)], d).wait()
+    here.all_of(hub_line.at[pl.ds(0, here.planes - 1)], e).wait()
+    whole = grad_line[0]
+    hub_sum = hub_line[0]
+    for i in range(1, here.planes):
+        whole = whole + grad_line[i]
+        hub_sum = hub_sum + hub_line[i]
+    grad_part[...] = whole
+    hub_sum_ref[...] = hub_sum
+    here.send_blocks(back_ref, halo_ref, c, 2 * third, 2 * third + 8)
+    kept = pltpu.make_async_copy(grad_part, whole_ref.at[here.p], keep.at[0])
+    kept.start()
+
+    def spread(i, _):
+        here.copy(grad_part, whole_ref.at[here.p], f, here.in_plane(i)[1]).start()
+        return 0
+
+    lax.fori_loop(1, PLANE, spread, 0)
+    here.send_blocks(back_ref, halo_ref, c, 2 * third + 8, here.count)
+    kept.wait()
+    here.all_of(whole_ref.at[pl.ds(0, PLANE - 1)], f).wait()
+    here.all_of(halo_ref.at[pl.ds(0, here.count - 1)], c).wait()
 
 
 def body(
@@ -239,7 +402,6 @@
     peers = lax.axis_size("vert")
     me = lax.axis_index("vert")
     slots = send_rows.shape[2]
-    depth = slots + HUB_MOST
     hub_total = hub_ids.shape[0]
     table_rows = local + peers * slots + hub_total
     edge_total = edge_src.shape[1]
@@ -257,13 +419,18 @@
     own_hubs = jnp.sum(jnp.where(picked, hub_local[None, :], 0), axis=1)
     own_back = jnp.where(lax.iota(jnp.int32, HUB_MOST) < own_count, own_hubs, local)
     before = jnp.sum((hub_owner[None, :] < hub_owner[:, None]).astype(jnp.int32), axis=1)
-    place = hub_owner * HUB_MOST + order - before
-
-    sent = pl.pallas_call(
+    planes = peers // PLANE
+    block = (hub_owner % PLANE) * planes + hub_owner // PLANE
+    place = block * HUB_MOST + order - before
+
+    sent, own_rows = pl.pallas_call(
         gather_kernel,
-        out_shape=jax.ShapeDtypeStruct((peers, depth, width), BF16),
+        out_shape=(
+            jax.ShapeDtypeStruct((peers, slots, width), BF16),
+            jax.ShapeDtypeStruct((HUB_MOST, width), BF16),
+        ),
         in_specs=[SMEM, SMEM, VMEM],
-        out_specs=VMEM,
+        out_specs=(VMEM, VMEM),
         scratch_shapes=[
             pltpu.VMEM((local, width), F32),
             pltpu.VMEM((peers * slots, width), F32),
@@ -271,7 +438,22 @@
         compiler_params=params,
         name="gather_sent",
     )(send, own_hubs, feats)
-    arrived = lax.all_to_all(sent, "vert", split_axis=0, concat_axis=0, tiled=True)
+    pair = pltpu.SemaphoreType.DMA((2,))
+    halo, hubs = pl.pallas_call(
+        forward_kernel,
+        out_shape=(
+            jax.ShapeDtypeStruct((peers, slots, width), BF16),
+            jax.ShapeDtypeStruct((PLANE, planes, HUB_MOST, width), BF16),
+        ),
+        in_specs=[VMEM, VMEM],
+        out_specs=(VMEM, VMEM),
+        scratch_shapes=[pair] * 4 + [pltpu.SemaphoreType.REGULAR],
+        compiler_params=pltpu.CompilerParams(
+            vmem_limit_bytes=LIMIT, collective_id=0, has_side_effects=True
+        ),
+        name="forward_exchange",
+    )(sent, own_rows)
+    hubs = hubs.reshape(peers, HUB_MOST, width)
 
     is_real = lax.iota(jnp.int32, edge_total) < edge_count[0]
     dst = jnp.where(is_real, edge_dst[0], local)
@@ -286,16 +468,17 @@
     inverse = jnp.broadcast_to((1.0 / jnp.maximum(degree, 1.0))[:, None], (local, width))
 
     rows_up = up(table_rows + 1, 64)
-    output, own, outgoing, grads = pl.pallas_call(
+    output, own, halo_back, hub_back, grads = pl.pallas_call(
         layer_kernel,
         out_shape=(
             jax.ShapeDtypeStruct((local, wide), BF16),
             jax.ShapeDtypeStruct((local, width), F32),
-            jax.ShapeDtypeStruct((peers, depth, width), BF16),
-            jax.ShapeDtypeStruct((2 * width + 8, wide), F32),
+            jax.ShapeDtypeStruct((peers, slots, width), BF16),
+            jax.ShapeDtypeStruct((peers, HUB_MOST, width), BF16),
+            jax.ShapeDtypeStruct((2 * width, wide + width), F32),
         ),
-        in_specs=[SMEM] * 4 + [VMEM] * 7,
-        out_specs=(VMEM,) * 4,
+        in_specs=[SMEM] * 4 + [VMEM] * 8,
+        out_specs=(VMEM,) * 5,
         scratch_shapes=[
             pltpu.VMEM((rows_up, width), F32),
             pltpu.VMEM((peers * HUB_MOST, width), F32),
@@ -304,25 +487,55 @@
         + [pltpu.VMEM((rows_up, width), F32)] * STREAMS,
         compiler_params=params,
         name="layer",
-    )(trips, src, dst, place, feats, arrived, inverse, cotangent, w_self, w_neigh, bias[None, :])
-
-    summed = lax.psum(grads, "vert")
-    returned = lax.all_to_all(outgoing, "vert", split_axis=0, concat_axis=0, tiled=True)
+    )(trips, src, dst, place, feats, halo, hubs, inverse, cotangent, w_self, w_neigh, bias[None, :])
+
+    piece = (2 * width // PLANE, wide + width)
+    returned, hub_sum, whole = pl.pallas_call(
+        backward_kernel,
+        out_shape=(
+            jax.ShapeDtypeStruct((peers, slots, width), BF16),
+            jax.ShapeDtypeStruct((HUB_MOST, width), F32),
+            jax.ShapeDtypeStruct((PLANE,) + piece, F32),
+        ),
+        in_specs=[VMEM] * 3,
+        out_specs=(VMEM,) * 3,
+        scratch_shapes=[
+            pltpu.VMEM((PLANE,) + piece, BF16),
+            pltpu.VMEM((PLANE, planes, HUB_MOST, width), BF16),
+            pltpu.VMEM((PLANE,) + piece, BF16),
+            pltpu.VMEM((planes, HUB_MOST, width), F32),
+            pltpu.VMEM((planes, HUB_MOST, width), F32),
+            pltpu.VMEM(piece, F32),
+            pltpu.VMEM((planes,) + piece, F32),
+        ]
+        + [pair] * 6
+        + [pltpu.SemaphoreType.DMA((3,)), pltpu.SemaphoreType.REGULAR],
+        compiler_params=pltpu.CompilerParams(
+            vmem_limit_bytes=LIMIT, collective_id=1, has_side_effects=True
+        ),
+        name="backward_exchange",
+    )(
+        halo_back,
+        hub_back.reshape(PLANE, planes, HUB_MOST, width),
+        grads.reshape((PLANE,) + piece),
+    )
+    whole = whole.reshape(2 * width, wide + width)
     grad_feats = pl.pallas_call(
         final_kernel,
         out_shape=jax.ShapeDtypeStruct((local, width), BF16),
-        in_specs=[SMEM, SMEM, VMEM, VMEM],
+        in_specs=[SMEM, SMEM, VMEM, VMEM, VMEM],
         out_specs=VMEM,
         scratch_shapes=[
             pltpu.VMEM((peers * slots, width), F32),
-            pltpu.VMEM((HUB_MOST, width), F32),
         ]
         + [pltpu.VMEM((up(local + 1, 8), width), F32)] * STREAMS,
         compiler_params=params,
         name="final",
-    )(send, own_back, own, returned)
-    grad_bias = jnp.sum(summed[2 * width :], axis=0)
-    return (output, grad_feats, summed[:width], summed[width : 2 * width], grad_bias)
+    )(send, own_back, own, returned, hub_sum)
+    grad_bias = jnp.concatenate(
+        [jnp.sum(whole[8 * j : 8 * j + 8, wide:], axis=0) for j in range(wide // width)]
+    )
+    return (output, grad_feats, whole[:width, :wide], whole[width:, :wide], grad_bias)
 
 
 def solution(mesh):

time: 424 us -> 164 us (0.39)
  waiting for transfers between devices: 298 us -> 0 us
  Pallas kernels: 73.8 us -> 146 us
  starting transfers between devices: 20.8 us -> 0 us
  between operations: 14.8 us -> 1.37 us
    psum x1 -> x0, waiting for transfers between devices: 270 us -> none  [body(): summed = lax.psum(grads, 'vert')]
    pallas_call x1 -> x3, Pallas kernels: 4.18 us -> 113 us  [the longest x1 77.6 us: body(): pl.pallas_call(backward_kernel, out_shape=(jax.ShapeDtypeStruct((peers, s...]
    pallas_call x1, Pallas kernels: 62.2 us -> 26.6 us  [body(): pl.pallas_call(layer_kernel, out_shape=(jax.ShapeDtypeStruct((local, wide...]
    all_to_all x2 -> x0, waiting for transfers between devices: 27.2 us -> none  [the longest x1 27.2 us: body(): lax.all_to_all(sent, 'vert', split_axis=0, concat_axis=0, tiled=True)]
    all_to_all x2 -> x0, starting transfers between devices: 20.8 us -> none  [the longest x1 14.7 us: body(): lax.all_to_all(sent, 'vert', split_axis=0, concat_axis=0, tiled=True)]
  transfers between devices with their start and end apart: 3 -> 0, of which waited for: 2 -> 0; matrix products, arithmetic and copies ran while one was open for 2% -> 0% of each run, Pallas kernels for 0% -> 0%
where the time goes in v2:
time: 164 us; the launch traced here: 161 us
  Pallas kernels  146 us (89%)
  other arithmetic  7.51 us (5%)
  local copies, waits for them, and re-layouts  3.63 us (2%)
  matrix products  2.34 us (1%)
    pallas_call x1, Pallas kernels, body(): pl.pallas_call(backward_kernel, out_shape=(jax.ShapeDtypeStruct((peers, s...  77.6 us
    pallas_call x1, Pallas kernels, body(): pl.pallas_call(forward_kernel, out_shape=(jax.ShapeDtypeStruct((peers, sl...  31.4 us
    pallas_call x1, Pallas kernels, body(): pl.pallas_call(layer_kernel, out_shape=(jax.ShapeDtypeStruct((local, wide...  26.6 us
    pallas_call x1, Pallas kernels, body(): pl.pallas_call(final_kernel, out_shape=jax.ShapeDtypeStruct((local, width...  6.95 us
    pallas_call x1, Pallas kernels, body(): pl.pallas_call(gather_kernel, out_shape=(jax.ShapeDtypeStruct((peers, slo...  3.96 us

profile of v2, /device:TPU:2, one launch (start us, length us, event | category | flops | bytes accessed | tf_op | source)
XLA Modules:
  0.0 161.3 jit_solution(6791065704559242)
XLA Ops:
  1.3 1.3 convert_reduce_fusion.1
  2.6 0.2 convert_reduce_fusion
  2.9 1.9 %convert_reduce_fusion.2 = (s32[]{:T(128)}, s32[368]{0:T(512)}, s32[368]{0:T(512)S(1)}) fusion(s32[368]{0:T(512)S(1)} %get-tuple-element.33, s32[]{:T(128)S(6)} %axis_index.12, s32[368]{0:T(512)S(1)} %convert_reduce_fusion, s32[368]{0:T(512)} %param.16), kind=kLoop, calls=%fused_computation.42 | loop fusion | flops 10671 | bytes 7368 | tf_op jit(solution)/shard_map/reduce_sum | solution.py:414
  4.8 0.6 iota_subtract_fusion
  5.4 0.1 select_reduce_fusion.hub_ref
  5.5 0.0 copy-start.2
  5.5 1.1 compare_select_fusion.hub_ref
  6.7 0.8 copy.16
  7.5 0.7 reshape.88.send_ref
  8.2 1.5 add_select_fusion.1
  9.8 0.0 copy-start
  9.8 2.3 %fusion.4 = f32[2048]{0:T(1024)S(1)} fusion(s32[16384]{0:T(1024)S(1)} %add_select_fusion, s32[16384]{0:T(1024)S(1)} %get-tuple-element.34), kind=kOutput, calls=%fused_computation.5 | convolution fusion | flops 69472256 | bytes 139264 | tf_op jit(solution)/shard_map/dot_general | solution.py:465
  12.1 0.0 copy-done.2
  12.1 0.0 copy-done
  12.1 4.0 %gather_sent.1 = (bf16[256,8,128]{2,1,0:T(8,128)(2,1)}, bf16[8,128]{1,0:T(8,128)(2,1)}) custom-call(s32[2048]{0:T(1024)} %reshape.88.send_ref, s32[8]{0:T(128)} %copy-done.2, bf16[2048,128]{1,0:T(8,128)(2,1)} %feats_ref.3), custom_call_target="tpu_custom_call" | custom-call | tf_op jit(solution)/shard_map/gather_sent/pallas_call | solution.py:426
  16.1 31.4 %forward_exchange.1 = (bf16[256,8,128]{2,1,0:T(8,128)(2,1)}, bf16[32,8,8,128]{3,2,1,0:T(8,128)(2,1)}) custom-call(bf16[256,8,128]{2,1,0:T(8,128)(2,1)} %get-tuple-element.17.sent_ref, bf16[8,128]{1,0:T(8,128)(2,1)} %get-tuple-element.18.hub_ref), custom_call_target="tpu_custom_call" | custom-call | tf_op jit(solution)/shard_map/forward_exchange/pallas_call | solution.py:442
  47.5 1.4 broadcast_in_dim.46.inverse_ref
  48.9 26.6 %layer.1 = (bf16[2048,256]{1,0:T(8,128)(2,1)}, f32[2048,128]{1,0:T(8,128)}, bf16[256,8,128]{2,1,0:T(8,128)(2,1)}, bf16[256,8,128]{2,1,0:T(8,128)(2,1)}, f32[256,384]{1,0:T(8,128)}) custom-call(s32[1]{0:T(128)S(6)} %select_n.54.trips_ref, s32[16384]{0:T(1024)} %get-tuple-element.41.src_ref, s32[16384]{0:T(1024)} %copy-done, s32[368]{0:T(512)} %get-tuple-element.39.place_ref, ...), custom_call_target="tpu_custom_call" | custom-call | tf_op jit(solution)/shard_map/layer/pallas_call | solution.py:471
  75.4 77.6 %backward_exchange.1 = (bf16[256,8,128]{2,1,0:T(8,128)(2,1)}, f32[8,128]{1,0:T(8,128)}, f32[32,8,384]{2,1,0:T(8,128)}) custom-call(bf16[256,8,128]{2,1,0:T(8,128)(2,1)} %get-tuple-element.23.back_ref, bf16[32,8,8,128]{3,2,1,0:T(8,128)(2,1)} %bitcast.12, f32[32,8,384]{2,1,0:T(8,128)} %bitcast.13), custom_call_target="tpu_custom_call" | custom-call | tf_op jit(solution)/shard_map/backward_exchange/pallas_call | solution.py:493
  153.1 0.0 copy-start.1
  153.1 6.9 %final.1 = bf16[2048,128]{1,0:T(8,128)(2,1)} custom-call(s32[2048]{0:T(1024)} %reshape.88.send_ref, s32[8]{0:T(128)} %compare_select_fusion.hub_ref, f32[2048,128]{1,0:T(8,128)} %get-tuple-element.22.own_ref, bf16[256,8,128]{2,1,0:T(8,128)(2,1)} %get-tuple-element.26.returned_ref, f32[8,128]{1,0:T(8,128)} %get-tuple-element.27.hub_sum), custom_call_target="tpu_custom_call" | custom-call | tf_op jit(solution)/shard_map/final/pallas_call | solution.py:523
  160.0 0.0 copy-done.1
  160.1 0.7 fusion.21
  160.8 0.6 pad_maximum_fusion
  (2 shorter events, 0.0 us)
Async XLA Ops:
  5.5 6.6 %copy-start.2 = (s32[8]{0:T(128)}, s32[8]{0:T(128)S(1)}, u32[]{:S(2)}) copy-start(s32[8]{0:T(128)S(1)} %select_reduce_fusion.hub_ref) | copy-start | bytes 100
  9.8 2.4 %copy-start = (s32[16384]{0:T(1024)}, s32[16384]{0:T(1024)S(1)}, u32[]{:S(2)}) copy-start(s32[16384]{0:T(1024)S(1)} %get-tuple-element.35.dst_ref) | copy-start | bytes 196612
  153.1 7.0 %copy-start.1 = (f32[32,8,384]{2,1,0:T(8,128)S(1)}, f32[32,8,384]{2,1,0:T(8,128)}, u32[]{:S(2)}) copy-start(f32[32,8,384]{2,1,0:T(8,128)} %get-tuple-element.28) | copy-start | bytes 1179652

commit v3 on v2

--- a/solution.py
+++ b/solution.py
@@ -9,8 +9,9 @@
 
 HUB_MOST = 8
 STREAMS = 8
-UNROLL = 4
-GROUP = STREAMS * UNROLL
+GROUP = 32
+CHUNK = 256
+WINDOW = 64
 LIMIT = 60 * 1024 * 1024
 F32 = jnp.float32
 BF16 = jnp.bfloat16
@@ -26,26 +27,17 @@
     return pl.ds(i, 1)
 
 
+def tile(i, step):
+    return pl.ds(pl.multiple_of(i * step, step), step)
+
+
 def clear(refs, rows, step):
     def some(i, _):
-        at = pl.ds(pl.multiple_of(i * step, step), step)
         for ref in refs:
-            ref[at, :] = jnp.zeros((step, ref.shape[1]), F32)
+            ref[tile(i, step), :] = jnp.zeros((step, ref.shape[1]), F32)
         return 0
 
     lax.fori_loop(0, rows // step, some, 0)
-
-
-def add_rows(trips, take, put, table, sums):
-    def some(i, _):
-        for j in range(GROUP):
-            e = i * GROUP + j
-            to = row(put[e])
-            ref = sums[j % STREAMS]
-            ref[to, :] = ref[to, :] + table[row(take[e]), :]
-        return 0
-
-    lax.fori_loop(0, trips, some, 0)
 
 
 def total(sums, at):
@@ -67,67 +59,150 @@
     lax.fori_loop(0, ref.shape[0] // blocks, some, 0)
 
 
-def gather_kernel(send_ref, hub_ref, feats_ref, out_ref, hub_out_ref, table, rows):
+def each_hub(hub_ref, local, planes, visit):
+    shift = local.bit_length() - 1
+
+    def some(i, carry):
+        last, offset = carry
+        for j in range(8):
+            h = i * 8 + j
+            owner = hub_ref[h] >> shift
+            offset = jnp.where(owner == last, offset + 1, 0)
+            block = lax.rem(owner, PLANE) * planes + lax.div(owner, PLANE)
+            visit(h, block * HUB_MOST + offset)
+            last = owner
+        return last, offset
+
+    lax.fori_loop(0, hub_ref.shape[0] // 8, some, (jnp.int32(-1), jnp.int32(0)))
+
+
+def gather_kernel(hub_ref, send_ref, feats_ref, out_ref, hub_out_ref, back_ref, table, rows):
     peers, slots, width = out_ref.shape
+    local = feats_ref.shape[0]
+    hubs = hub_ref.shape[0]
     table[...] = feats_ref[...].astype(F32)
 
     def some(i, _):
         for j in range(GROUP):
-            e = i * GROUP + j
-            rows[row(e), :] = table[row(send_ref[e]), :]
+            p, c = i * (GROUP // slots) + j // slots, j % slots
+            rows[row(i * GROUP + j), :] = table[row(send_ref[c, p]), :]
         return 0
 
     lax.fori_loop(0, peers * slots // GROUP, some, 0)
-    hubs = jnp.concatenate([table[row(hub_ref[j]), :] for j in range(HUB_MOST)], axis=0)
-    hub_out_ref[...] = hubs.astype(BF16)
+    start = lax.axis_index("vert") * local
+
+    def look(i, carry):
+        first, after = carry
+        for j in range(8):
+            at = hub_ref[i * 8 + j] - start
+            first = first + (at < 0).astype(jnp.int32)
+            after = after + (at < local).astype(jnp.int32)
+        return first, after
+
+    first, after = lax.fori_loop(0, hubs // 8, look, (jnp.int32(0), jnp.int32(0)))
+    own = []
+    for j in range(HUB_MOST):
+        here = jnp.minimum(first + j, jnp.maximum(after - 1, 0))
+        at = jnp.clip(hub_ref[here] - start, 0, local - 1)
+        own.append(table[row(at), :])
+        back_ref[j] = jnp.where(first + j < after, at, local)
+    hub_out_ref[...] = jnp.concatenate(own, axis=0).astype(BF16)
 
     def pack(i, _):
-        at = pl.multiple_of(i * 16 * slots, 8)
-        own = rows[pl.ds(at, 16 * slots), :].reshape(16, slots, width).astype(BF16)
-        out_ref[pl.ds(i * 16, 16)] = own
+        part = rows[tile(i, 16 * slots), :].reshape(16, slots, width).astype(BF16)
+        out_ref[pl.ds(i * 16, 16)] = part
         return 0
 
     lax.fori_loop(0, peers // 16, pack, 0)
 
 
+def one_hot(lanes_ref, c, base, count):
+    halves = []
+    for h in range(CHUNK // 128):
+        r = c * (CHUNK // 128) + h
+        ends = lanes_ref[row(r), :] - base
+        e = r * 128 + lax.broadcasted_iota(jnp.int32, (1, 128), 1)
+        ends = jnp.where(e < count, ends, -1)
+        hit = lax.broadcasted_iota(jnp.int32, (WINDOW, 128), 0) == ends
+        halves.append(jnp.where(hit, 1.0, 0.0).astype(BF16))
+    return jnp.concatenate(halves, axis=1)
+
+
 def layer_kernel(
-    trips_ref, src_ref, dst_ref, place_ref,
-    feats_ref, halo_ref, hubs_ref, inverse_ref, cot_ref, w_self_ref, w_neigh_ref, bias_ref,
+    count_ref, src_ref, dst_ref, hub_ref,
+    lanes_ref, feats_ref, halo_ref, hubs_ref, cot_ref, w_self_ref, w_neigh_ref, bias_ref,
     out_ref, own_ref, halo_back_ref, hub_back_ref, grads_ref,
-    table, hub_slots, spread, *sums,
+    table, hub_slots, spread, summed, degrees, even, odd, *sums,
 ):
     local, width = feats_ref.shape
     peers, slots, _ = halo_ref.shape
-    hubs = place_ref.shape[0]
+    hubs = hub_ref.shape[0]
     wide = w_self_ref.shape[1]
     halo_end = local + peers * slots
-    trips = trips_ref[0]
+    last_chunk = src_ref.shape[0] // CHUNK - 1
+    count = count_ref[0]
+    pairs = lax.div(count + (2 * CHUNK - 1), 2 * CHUNK)
     step = 256
-
-    clear(sums, up(local + 1, 64), 64)
+    outer = (((0,), (0,)), ((), ()))
+    back = (((1,), (1,)), ((), ()))
+
+    def base_of(c):
+        return lax.shift_left(lax.shift_right_logical(dst_ref[c * CHUNK], 3), 3)
+
+    def windows_of(c):
+        return lax.div(dst_ref[c * CHUNK + CHUNK - 1] - base_of(c), WINDOW) + 1
+
+    clear((summed, degrees), summed.shape[0], WINDOW)
     table[:local, :] = feats_ref[...].astype(F32)
     widen(halo_ref, table, local)
     widen(hubs_ref, hub_slots, 0)
 
-    def hub_in(i, _):
-        for j in range(8):
-            h = i * 8 + j
-            table[row(halo_end + h), :] = hub_slots[row(place_ref[h]), :]
-        return 0
-
-    lax.fori_loop(0, hubs // 8, hub_in, 0)
-    add_rows(trips, src_ref, dst_ref, table, sums)
+    def hub_in(h, slot):
+        table[row(halo_end + h), :] = hub_slots[row(slot), :]
+
+    each_hub(hub_ref, local, peers // PLANE, hub_in)
+
+    def fetch(c, rows):
+        for j in range(CHUNK):
+            rows[j : j + 1, :] = table[row(src_ref[c * CHUNK + j]), :]
+
+    def reduce(c, rows, k):
+        base = pl.multiple_of(base_of(c) + k * WINDOW, 8)
+        at = pl.ds(base, WINDOW)
+        right = jnp.concatenate([rows[...].astype(BF16), jnp.ones((CHUNK, width), BF16)], axis=1)
+        part = jnp.dot(one_hot(lanes_ref, c, base, count), right, preferred_element_type=F32)
+        summed[at, :] += part[:, :width]
+        degrees[at, :] += part[:, width:]
+
+    def reduce_more(c, rows):
+        def some(k, _):
+            reduce(c, rows, k)
+            return 0
+
+        lax.fori_loop(1, windows_of(c), some, 0)
+
+    fetch(0, even)
+
+    def forward(i, _):
+        c = 2 * i
+        reduce(c, even, 0)
+        fetch(c + 1, odd)
+        reduce_more(c, even)
+        reduce(c + 1, odd, 0)
+        fetch(jnp.minimum(c + 2, last_chunk), even)
+        reduce_more(c + 1, odd)
+        return 0
+
+    lax.fori_loop(0, pairs, forward, 0)
 
     grads_ref[...] = jnp.zeros_like(grads_ref)
     w_self, w_neigh, bias = w_self_ref[...], w_neigh_ref[...], bias_ref[...]
-    outer = (((0,), (0,)), ((), ()))
-    back = (((1,), (1,)), ((), ()))
 
     def dense(i, _):
-        at = pl.ds(pl.multiple_of(i * step, step), step)
+        at = tile(i, step)
         feats = feats_ref[at, :]
-        inverse = inverse_ref[at, :]
-        mean = (total(sums, at) * inverse).astype(BF16)
+        inverse = 1.0 / jnp.maximum(degrees[at, :], 1.0)
+        mean = (summed[at, :] * inverse).astype(BF16)
         linear = jnp.dot(feats, w_self, preferred_element_type=F32)
         linear = linear + jnp.dot(mean, w_neigh, preferred_element_type=F32) + bias
         logistic = jax.nn.sigmoid(linear)
@@ -148,11 +223,52 @@
     lax.fori_loop(0, local // step, dense, 0)
 
     clear(sums, sums[0].shape[0], 64)
-    spread[local : local + 8, :] = jnp.zeros((8, width), F32)
-    add_rows(trips, dst_ref, src_ref, spread, sums)
+    spread[local:, :] = jnp.zeros((spread.shape[0] - local, width), F32)
+
+    def expand(c, k):
+        base = pl.multiple_of(base_of(c) + k * WINDOW, 8)
+        values = spread[pl.ds(base, WINDOW), :]
+        high = values.astype(BF16)
+        low = (values - high.astype(F32)).astype(BF16)
+        both = lax.dot_general(
+            one_hot(lanes_ref, c, base, count),
+            jnp.concatenate([high, low], axis=1),
+            outer,
+            preferred_element_type=F32,
+        )
+        return both[:, :width] + both[:, width:]
+
+    def expand_more(c, rows):
+        def some(k, _):
+            rows[...] += expand(c, k)
+            return 0
+
+        lax.fori_loop(1, windows_of(c), some, 0)
+
+    def update(c, rows):
+        for j in range(CHUNK):
+            to = row(src_ref[c * CHUNK + j])
+            ref = sums[j % STREAMS]
+            ref[to, :] = ref[to, :] + rows[j : j + 1, :]
+
+    even[...] = expand(0, 0)
+    expand_more(0, even)
+
+    def backward(i, _):
+        c = 2 * i
+        odd[...] = expand(c + 1, 0)
+        update(c, even)
+        expand_more(c + 1, odd)
+        after = jnp.minimum(c + 2, last_chunk)
+        even[...] = expand(after, 0)
+        update(c + 1, odd)
+        expand_more(after, even)
+        return 0
+
+    lax.fori_loop(0, pairs, backward, 0)
 
     def own_part(i, _):
-        at = pl.ds(pl.multiple_of(i * step, step), step)
+        at = tile(i, step)
         own_ref[at, :] += total(sums, at)
         return 0
 
@@ -170,53 +286,50 @@
 
     def hub_part(i, _):
         at = pl.ds(pl.multiple_of(halo_end + i * 8, 8), 8)
-        table[pl.ds(pl.multiple_of(i * 8, 8), 8), :] = total(sums, at)
+        table[tile(i, 8), :] = total(sums, at)
         return 0
 
     lax.fori_loop(0, hubs // 8, hub_part, 0)
 
-    def hub_out(i, _):
-        for j in range(8):
-            h = i * 8 + j
-            hub_slots[row(place_ref[h]), :] = table[row(h), :]
-        return 0
-
-    lax.fori_loop(0, hubs // 8, hub_out, 0)
+    def hub_out(h, slot):
+        hub_slots[row(slot), :] = table[row(h), :]
+
+    each_hub(hub_ref, local, peers // PLANE, hub_out)
 
     def hub_pack(i, _):
-        at = pl.ds(pl.multiple_of(i * 16 * HUB_MOST, 8), 16 * HUB_MOST)
-        part = hub_slots[at, :].reshape(16, HUB_MOST, width).astype(BF16)
+        part = hub_slots[tile(i, 16 * HUB_MOST), :].reshape(16, HUB_MOST, width).astype(BF16)
         hub_back_ref[pl.ds(i * 16, 16)] = part
         return 0
 
     lax.fori_loop(0, peers // 16, hub_pack, 0)
 
 
-def final_kernel(send_ref, hub_ref, own_ref, returned_ref, hub_sum, out_ref, rows, *sums):
+def final_kernel(hub_ref, send_ref, own_ref, returned_ref, hub_sum, out_ref, rows, parts, sums):
     peers, slots, width = returned_ref.shape
     local = own_ref.shape[0]
     step = 256
-    sums[0][:local, :] = own_ref[...]
-    clear(sums[1:], up(local + 1, 8), 8)
     widen(returned_ref, rows, 0)
+    for c in range(slots):
+        parts[c] = rows[pl.ds(c, peers, stride=slots), :].astype(BF16)
 
     def some(i, _):
-        for j in range(GROUP):
-            e = i * GROUP + j
-            to = row(send_ref[e])
-            ref = sums[j % STREAMS]
-            ref[to, :] = ref[to, :] + rows[row(e), :]
-        return 0
-
-    lax.fori_loop(0, peers * slots // GROUP, some, 0)
-
+        at = tile(i, step)
+        acc = own_ref[at, :]
+        for c in range(slots):
+            ends = send_ref[c : c + 1, :] - i * step
+            hit = lax.broadcasted_iota(jnp.int32, (step, peers), 0) == ends
+            pick = jnp.where(hit, 1.0, 0.0).astype(BF16)
+            acc = acc + jnp.dot(pick, parts[c], preferred_element_type=F32)
+        sums[at, :] = acc
+        return 0
+
+    lax.fori_loop(0, local // step, some, 0)
     for j in range(HUB_MOST):
         to = row(hub_ref[j])
-        sums[0][to, :] = sums[0][to, :] + hub_sum[row(j), :]
+        sums[to, :] = sums[to, :] + hub_sum[j : j + 1, :]
 
     def close(i, _):
-        at = pl.ds(pl.multiple_of(i * step, step), step)
-        out_ref[at, :] = total(sums, at).astype(BF16)
+        out_ref[tile(i, step), :] = sums[tile(i, step), :].astype(BF16)
         return 0
 
     lax.fori_loop(0, local // step, close, 0)
@@ -400,44 +513,30 @@
     local, width = feats.shape
     wide = w_self.shape[1]
     peers = lax.axis_size("vert")
-    me = lax.axis_index("vert")
     slots = send_rows.shape[2]
     hub_total = hub_ids.shape[0]
     table_rows = local + peers * slots + hub_total
-    edge_total = edge_src.shape[1]
     params = pltpu.CompilerParams(vmem_limit_bytes=LIMIT)
 
-    send = send_rows.reshape(-1)
-    hub_owner = hub_ids // local
-    hub_local = hub_ids - hub_owner * local
-    order = lax.iota(jnp.int32, hub_total)
-    first = jnp.sum((hub_owner < me).astype(jnp.int32))
-    picked = (hub_owner == me)[None, :] & (
-        (order - first)[None, :] == lax.iota(jnp.int32, HUB_MOST)[:, None]
-    )
-    own_count = jnp.sum((hub_owner == me).astype(jnp.int32))
-    own_hubs = jnp.sum(jnp.where(picked, hub_local[None, :], 0), axis=1)
-    own_back = jnp.where(lax.iota(jnp.int32, HUB_MOST) < own_count, own_hubs, local)
-    before = jnp.sum((hub_owner[None, :] < hub_owner[:, None]).astype(jnp.int32), axis=1)
+    send = send_rows[0].T
     planes = peers // PLANE
-    block = (hub_owner % PLANE) * planes + hub_owner // PLANE
-    place = block * HUB_MOST + order - before
-
-    sent, own_rows = pl.pallas_call(
+
+    sent, own_rows, own_back = pl.pallas_call(
         gather_kernel,
         out_shape=(
             jax.ShapeDtypeStruct((peers, slots, width), BF16),
             jax.ShapeDtypeStruct((HUB_MOST, width), BF16),
+            jax.ShapeDtypeStruct((HUB_MOST,), jnp.int32),
         ),
         in_specs=[SMEM, SMEM, VMEM],
-        out_specs=(VMEM, VMEM),
+        out_specs=(VMEM, VMEM, SMEM),
         scratch_shapes=[
             pltpu.VMEM((local, width), F32),
             pltpu.VMEM((peers * slots, width), F32),
         ],
         compiler_params=params,
         name="gather_sent",
-    )(send, own_hubs, feats)
+    )(hub_ids, send, feats)
     pair = pltpu.SemaphoreType.DMA((2,))
     halo, hubs = pl.pallas_call(
         forward_kernel,
@@ -455,19 +554,7 @@
     )(sent, own_rows)
     hubs = hubs.reshape(peers, HUB_MOST, width)
 
-    is_real = lax.iota(jnp.int32, edge_total) < edge_count[0]
-    dst = jnp.where(is_real, edge_dst[0], local)
-    src = jnp.where(is_real, edge_src[0], table_rows)
-    trips = (edge_count + (GROUP - 1)) // GROUP
-    lanes = 128
-    high = (dst // lanes)[:, None] == lax.iota(jnp.int32, local // lanes)[None, :]
-    low = (dst % lanes)[:, None] == lax.iota(jnp.int32, lanes)[None, :]
-    degree = lax.dot_general(
-        high.astype(BF16), low.astype(BF16), (((0,), (0,)), ((), ())), preferred_element_type=F32
-    ).reshape(-1)
-    inverse = jnp.broadcast_to((1.0 / jnp.maximum(degree, 1.0))[:, None], (local, width))
-
-    rows_up = up(table_rows + 1, 64)
+    rows_up = up(table_rows, 64)
     output, own, halo_back, hub_back, grads = pl.pallas_call(
         layer_kernel,
         out_shape=(
@@ -482,12 +569,16 @@
         scratch_shapes=[
             pltpu.VMEM((rows_up, width), F32),
             pltpu.VMEM((peers * HUB_MOST, width), F32),
-            pltpu.VMEM((up(local + 1, 8), width), F32),
         ]
+        + [pltpu.VMEM((local + WINDOW, width), F32)] * 3
+        + [pltpu.VMEM((CHUNK, width), F32)] * 2
         + [pltpu.VMEM((rows_up, width), F32)] * STREAMS,
         compiler_params=params,
         name="layer",
-    )(trips, src, dst, place, feats, halo, hubs, inverse, cotangent, w_self, w_neigh, bias[None, :])
+    )(
+        edge_count, edge_src[0], edge_dst[0], hub_ids, edge_dst.reshape(-1, 128), feats,
+        halo, hubs, cotangent, w_self, w_neigh, bias[None, :],
+    )
 
     piece = (2 * width // PLANE, wide + width)
     returned, hub_sum, whole = pl.pallas_call(
@@ -523,15 +614,16 @@
     grad_feats = pl.pallas_call(
         final_kernel,
         out_shape=jax.ShapeDtypeStruct((local, width), BF16),
-        in_specs=[SMEM, SMEM, VMEM, VMEM, VMEM],
+        in_specs=[SMEM] + [VMEM] * 4,
         out_specs=VMEM,
         scratch_shapes=[
             pltpu.VMEM((peers * slots, width), F32),
-        ]
-        + [pltpu.VMEM((up(local + 1, 8), width), F32)] * STREAMS,
+            pltpu.VMEM((slots, peers, width), BF16),
+            pltpu.VMEM((up(local + 1, 8), width), F32),
+        ],
         compiler_params=params,
         name="final",
-    )(send, own_back, own, returned, hub_sum)
+    )(own_back, send, own, returned, hub_sum)
     grad_bias = jnp.concatenate(
         [jnp.sum(whole[8 * j : 8 * j + 8, wide:], axis=0) for j in range(wide // width)]
     )

time: 164 us -> 142 us (0.87)
  Pallas kernels: 146 us -> 138 us
  other arithmetic: 7.51 us -> 0.58 us
  local copies, waits for them, and re-layouts: 3.63 us -> 0.72 us
  matrix products: 2.34 us -> 0 us
    pallas_call x1, Pallas kernels: 77.6 us -> 67.1 us  [body(): pl.pallas_call(backward_kernel, out_shape=(jax.ShapeDtypeStruct((peers, s...]
    reduce_sum x4 -> x0, other arithmetic: 3.58 us -> none  [the longest x1 1.9 us: body(): first = jnp.sum((hub_owner < me).astype(jnp.int32))]
    select_n x3 -> x0, other arithmetic: 2.7 us -> none  [the longest x1 1.54 us: body(): dst // lanes]
    dot_general x1 -> x0, matrix products: 2.34 us -> none  [body(): lax.dot_general(high.astype(BF16), low.astype(BF16), (((0,), (0,)), ((),...]
    pallas_call x1, Pallas kernels: 3.96 us -> 6 us  [body(): pl.pallas_call(gather_kernel, out_shape=(jax.ShapeDtypeStruct((peers, slo...]
where the time goes in v3:
time: 142 us; the launch traced here: 141 us
  Pallas kernels  138 us (97%)
    pallas_call x1, Pallas kernels, body(): pl.pallas_call(backward_kernel, out_shape=(jax.ShapeDtypeStruct((peers, s...  67.1 us
    pallas_call x1, Pallas kernels, body(): pl.pallas_call(forward_kernel, out_shape=(jax.ShapeDtypeStruct((peers, sl...  31.5 us
    pallas_call x1, Pallas kernels, body(): pl.pallas_call(layer_kernel, out_shape=(jax.ShapeDtypeStruct((local, wide...  27.7 us
    pallas_call x1, Pallas kernels, body(): pl.pallas_call(final_kernel, out_shape=jax.ShapeDtypeStruct((local, width...  6.04 us
    pallas_call x1, Pallas kernels, body(): pl.pallas_call(gather_kernel, out_shape=(jax.ShapeDtypeStruct((peers, slo...  6 us

profile of v3, /device:TPU:2, one launch (start us, length us, event | category | flops | bytes accessed | tf_op | source)
XLA Modules:
  0.0 140.9 jit_solution(12470344421723687963)
XLA Ops:
  1.3 6.0 %gather_sent.1 = (bf16[256,8,128]{2,1,0:T(8,128)(2,1)}, bf16[8,128]{1,0:T(8,128)(2,1)}, s32[8]{0:T(128)}) custom-call(s32[368]{0:T(512)} %hub_ref.3, s32[8,256]{1,0:T(8,128)} %bitcast.19, bf16[2048,128]{1,0:T(8,128)(2,1)} %feats_ref.3), custom_call_target="tpu_custom_call" | custom-call | tf_op jit(solution)/shard_map/gather_sent/pallas_call | solution.py:524
  7.3 31.5 %forward_exchange.1 = (bf16[256,8,128]{2,1,0:T(8,128)(2,1)}, bf16[32,8,8,128]{3,2,1,0:T(8,128)(2,1)}) custom-call(bf16[256,8,128]{2,1,0:T(8,128)(2,1)} %get-tuple-element.18.sent_ref, bf16[8,128]{1,0:T(8,128)(2,1)} %get-tuple-element.19.hub_ref), custom_call_target="tpu_custom_call" | custom-call | tf_op jit(solution)/shard_map/forward_exchange/pallas_call | solution.py:541
  38.8 27.7 %layer.1 = (bf16[2048,256]{1,0:T(8,128)(2,1)}, f32[2048,128]{1,0:T(8,128)}, bf16[256,8,128]{2,1,0:T(8,128)(2,1)}, bf16[256,8,128]{2,1,0:T(8,128)(2,1)}, f32[256,384]{1,0:T(8,128)}) custom-call(s32[1]{0:T(128)S(6)} %copy.15.count_ref, s32[16384]{0:T(1024)} %bitcast.18, s32[16384]{0:T(1024)} %bitcast.14, s32[368]{0:T(512)} %hub_ref.3, s32[128,128]{1,0:T(8,128)} %bitcast.15, ...), custom_call_target="tpu_custom_call" | custom-call | tf_op jit(solution)/shard_map/layer/pallas_call | solution.py:558
  66.5 67.1 %backward_exchange.1 = (bf16[256,8,128]{2,1,0:T(8,128)(2,1)}, f32[8,128]{1,0:T(8,128)}, f32[32,8,384]{2,1,0:T(8,128)}) custom-call(bf16[256,8,128]{2,1,0:T(8,128)(2,1)} %get-tuple-element.25.back_ref, bf16[32,8,8,128]{3,2,1,0:T(8,128)(2,1)} %bitcast.11, f32[32,8,384]{2,1,0:T(8,128)} %bitcast.13), custom_call_target="tpu_custom_call" | custom-call | tf_op jit(solution)/shard_map/backward_exchange/pallas_call | solution.py:584
  133.6 0.0 copy-start
  133.6 6.0 %final.1 = bf16[2048,128]{1,0:T(8,128)(2,1)} custom-call(s32[8]{0:T(128)} %get-tuple-element.23.hub_ref, s32[8,256]{1,0:T(8,128)} %bitcast.20, f32[2048,128]{1,0:T(8,128)} %get-tuple-element.24.own_ref, bf16[256,8,128]{2,1,0:T(8,128)(2,1)} %get-tuple-element.28.returned_ref, f32[8,128]{1,0:T(8,128)} %get-tuple-element.29.hub_sum), custom_call_target="tpu_custom_call" | custom-call | tf_op jit(solution)/shard_map/final/pallas_call | solution.py:614
  139.6 0.0 copy-done
  139.6 0.7 fusion
  140.4 0.6 pad_maximum_fusion
  (1 shorter events, 0.0 us)
Async XLA Ops:
  133.6 6.1 %copy-start = (f32[32,8,384]{2,1,0:T(8,128)S(1)}, f32[32,8,384]{2,1,0:T(8,128)}, u32[]{:S(2)}) copy-start(f32[32,8,384]{2,1,0:T(8,128)} %get-tuple-element.30) | copy-start | bytes 1179652

commit v4 on v3

--- a/solution.py
+++ b/solution.py
@@ -12,6 +12,8 @@
 GROUP = 32
 CHUNK = 256
 WINDOW = 64
+FIRST = 168
+SECOND = 232
 LIMIT = 60 * 1024 * 1024
 F32 = jnp.float32
 BF16 = jnp.bfloat16
@@ -106,6 +108,7 @@
         at = jnp.clip(hub_ref[here] - start, 0, local - 1)
         own.append(table[row(at), :])
         back_ref[j] = jnp.where(first + j < after, at, local)
+    back_ref[HUB_MOST] = first
     hub_out_ref[...] = jnp.concatenate(own, axis=0).astype(BF16)
 
     def pack(i, _):
@@ -131,7 +134,7 @@
 def layer_kernel(
     count_ref, src_ref, dst_ref, hub_ref,
     lanes_ref, feats_ref, halo_ref, hubs_ref, cot_ref, w_self_ref, w_neigh_ref, bias_ref,
-    out_ref, own_ref, halo_back_ref, hub_back_ref, grads_ref,
+    out_ref, own_ref, halo_back_ref, grads_ref,
     table, hub_slots, spread, summed, degrees, even, odd, *sums,
 ):
     local, width = feats_ref.shape
@@ -215,7 +218,7 @@
         )
         grad_sum = jnp.sum(grad.astype(F32).reshape(step // 8, 8, wide), axis=0)
         for j in range(wide // width):
-            grads_ref[8 * j : 8 * j + 8, wide:] += grad_sum[:, j * width : (j + 1) * width]
+            grads_ref[8 * j : 8 * j + 8, wide : wide + width] += grad_sum[:, j * width : (j + 1) * width]
         own_ref[at, :] = lax.dot_general(grad, w_self, back, preferred_element_type=F32)
         spread[at, :] = lax.dot_general(grad, w_neigh, back, preferred_element_type=F32) * inverse
         return 0
@@ -282,29 +285,17 @@
 
     lax.fori_loop(0, peers // 16, halo_part, 0)
 
-    clear((hub_slots,), peers * HUB_MOST, 64)
-
     def hub_part(i, _):
-        at = pl.ds(pl.multiple_of(halo_end + i * 8, 8), 8)
-        table[tile(i, 8), :] = total(sums, at)
-        return 0
-
-    lax.fori_loop(0, hubs // 8, hub_part, 0)
-
-    def hub_out(h, slot):
-        hub_slots[row(slot), :] = table[row(h), :]
-
-    each_hub(hub_ref, local, peers // PLANE, hub_out)
-
-    def hub_pack(i, _):
-        part = hub_slots[tile(i, 16 * HUB_MOST), :].reshape(16, HUB_MOST, width).astype(BF16)
-        hub_back_ref[pl.ds(i * 16, 16)] = part
-        return 0
-
-    lax.fori_loop(0, peers // 16, hub_pack, 0)
-
-
-def final_kernel(hub_ref, send_ref, own_ref, returned_ref, hub_sum, out_ref, rows, parts, sums):
+        for j in range(2):
+            at = pl.ds(pl.multiple_of(halo_end + i * 16 + j * 8, 8), 8)
+            lanes = wide + (1 + j) * width
+            grads_ref[tile(i, 8), lanes : lanes + width] = total(sums, at)
+        return 0
+
+    lax.fori_loop(0, hubs // 16, hub_part, 0)
+
+
+def final_kernel(hub_ref, send_ref, own_ref, returned_ref, whole_ref, out_ref, rows, parts, sums):
     peers, slots, width = returned_ref.shape
     local = own_ref.shape[0]
     step = 256
@@ -324,9 +315,13 @@
         return 0
 
     lax.fori_loop(0, local // step, some, 0)
+    lanes = whole_ref.shape[1] - 2 * width
     for j in range(HUB_MOST):
         to = row(hub_ref[j])
-        sums[to, :] = sums[to, :] + hub_sum[j : j + 1, :]
+        h = hub_ref[HUB_MOST] + j
+        both = whole_ref[row(lax.div(h, 16) * 8 + lax.rem(h, 8)), lanes:]
+        late = lax.rem(h, 16) >= 8
+        sums[to, :] = sums[to, :] + jnp.where(late, both[:, width:], both[:, :width])
 
     def close(i, _):
         out_ref[tile(i, step), :] = sums[tile(i, step), :].astype(BF16)
@@ -431,80 +426,61 @@
 
 
 def backward_kernel(
-    back_ref, hub_ref, grads_ref, halo_ref, hub_sum_ref, whole_ref,
-    part_in, hub_in, grads_in, hub_part, hub_line, grad_part, grad_line,
-    a, b, c, d, e, f, keep, ready,
+    back_ref, grads_ref, halo_ref, whole_ref, part_in, parts, part, line, a, b, c, d, keep, ready
 ):
     here = Places()
     part_in[...] = grads_ref[...].astype(BF16)
     here.barrier(ready)
     kept = [
         pltpu.make_async_copy(back_ref.at[here.me], halo_ref.at[here.me], keep.at[0]),
-        pltpu.make_async_copy(hub_ref.at[here.p], hub_in.at[here.p], keep.at[1]),
-        pltpu.make_async_copy(part_in.at[here.p], grads_in.at[here.p], keep.at[2]),
+        pltpu.make_async_copy(part_in.at[here.p], parts.at[here.p], keep.at[1]),
     ]
     for copy in kept:
         copy.start()
 
     def across(i, _):
         p, to = here.in_plane(i)
-        here.copy(part_in.at[p], grads_in.at[here.p], a, to).start()
-        here.copy(hub_ref.at[p], hub_in.at[here.p], b, to).start()
+        here.copy(part_in.at[p], parts.at[here.p], a, to).start()
         return 0
 
     lax.fori_loop(1, PLANE, across, 0)
-    third = here.count // 3
-    here.send_blocks(back_ref, halo_ref, c, 0, third)
+    early, later = here.count * FIRST // 256, here.count * SECOND // 256
+    here.send_blocks(back_ref, halo_ref, b, 0, early)
     for copy in kept:
         copy.wait()
-    here.all_of(grads_in.at[pl.ds(0, PLANE - 1)], a).wait()
-    here.all_of(hub_in.at[pl.ds(0, PLANE - 1)], b).wait()
-    grad_part[...] = lax.fori_loop(
-        0, PLANE, lambda i, acc: acc + grads_in[i].astype(F32), jnp.zeros(grad_part.shape, F32)
+    here.all_of(parts.at[pl.ds(0, PLANE - 1)], a).wait()
+    part[...] = lax.fori_loop(
+        0, PLANE, lambda i, acc: acc + parts[i].astype(F32), jnp.zeros(part.shape, F32)
     )
-    hub_part[...] = lax.fori_loop(
-        0, PLANE, lambda i, acc: acc + hub_in[i].astype(F32), jnp.zeros(hub_part.shape, F32)
-    )
-    here.send_blocks(back_ref, halo_ref, c, third, third + 8)
-    kept = [
-        pltpu.make_async_copy(grad_part, grad_line.at[here.z], keep.at[0]),
-        pltpu.make_async_copy(hub_part.at[here.z], hub_line.at[here.z], keep.at[1]),
-    ]
-    for copy in kept:
-        copy.start()
+    here.send_blocks(back_ref, halo_ref, b, early, early + 8)
+    kept = pltpu.make_async_copy(part, line.at[here.z], keep.at[0])
+    kept.start()
 
     def along(i, _):
-        z, to = here.in_line(i)
-        here.copy(grad_part, grad_line.at[here.z], d, to).start()
-        here.copy(hub_part.at[z], hub_line.at[here.z], e, to).start()
+        here.copy(part, line.at[here.z], c, here.in_line(i)[1]).start()
         return 0
 
     lax.fori_loop(1, here.planes, along, 0)
-    here.send_blocks(back_ref, halo_ref, c, third + 8, 2 * third)
-    for copy in kept:
-        copy.wait()
-    here.all_of(grad_line.at[pl.ds(0, here.planes - 1)], d).wait()
-    here.all_of(hub_line.at[pl.ds(0, here.planes - 1)], e).wait()
-    whole = grad_line[0]
-    hub_sum = hub_line[0]
+    here.send_blocks(back_ref, halo_ref, b, early + 8, later)
+    kept.wait()
+    here.all_of(line.at[pl.ds(0, here.planes - 1)], c).wait()
+    whole = line[0]
     for i in range(1, here.planes):
-        whole = whole + grad_line[i]
-        hub_sum = hub_sum + hub_line[i]
-    grad_part[...] = whole
-    hub_sum_ref[...] = hub_sum
-    here.send_blocks(back_ref, halo_ref, c, 2 * third, 2 * third + 8)
-    kept = pltpu.make_async_copy(grad_part, whole_ref.at[here.p], keep.at[0])
+        whole = whole + line[i]
+    part[...] = whole
+    here.send_blocks(back_ref, halo_ref, b, later, later + 8)
+    kept = pltpu.make_async_copy(part, whole_ref.at[here.p], keep.at[0])
     kept.start()
 
     def spread(i, _):
-        here.copy(grad_part, whole_ref.at[here.p], f, here.in_plane(i)[1]).start()
+        here.copy(part, whole_ref.at[here.p], d, here.in_plane(i)[1]).start()
         return 0
 
     lax.fori_loop(1, PLANE, spread, 0)
-    here.send_blocks(back_ref, halo_ref, c, 2 * third + 8, here.count)
+    here.send_blocks(back_ref, halo_ref, b, later + 8, here.count)
     kept.wait()
-    here.all_of(whole_ref.at[pl.ds(0, PLANE - 1)], f).wait()
-    here.all_of(halo_ref.at[pl.ds(0, here.count - 1)], c).wait()
+    here.all_of(whole_ref.at[pl.ds(0, PLANE - 1)], d).wait()
+    here.all_of(halo_ref.at[pl.ds(0, here.count - 1)], b).wait()
 
 
 def body(
@@ -526,7 +502,7 @@
         out_shape=(
             jax.ShapeDtypeStruct((peers, slots, width), BF16),
             jax.ShapeDtypeStruct((HUB_MOST, width), BF16),
-            jax.ShapeDtypeStruct((HUB_MOST,), jnp.int32),
+            jax.ShapeDtypeStruct((HUB_MOST + 1,), jnp.int32),
         ),
         in_specs=[SMEM, SMEM, VMEM],
         out_specs=(VMEM, VMEM, SMEM),
@@ -555,17 +531,16 @@
     hubs = hubs.reshape(peers, HUB_MOST, width)
 
     rows_up = up(table_rows, 64)
-    output, own, halo_back, hub_back, grads = pl.pallas_call(
+    output, own, halo_back, grads = pl.pallas_call(
         layer_kernel,
         out_shape=(
             jax.ShapeDtypeStruct((local, wide), BF16),
             jax.ShapeDtypeStruct((local, width), F32),
             jax.ShapeDtypeStruct((peers, slots, width), BF16),
-            jax.ShapeDtypeStruct((peers, HUB_MOST, width), BF16),
-            jax.ShapeDtypeStruct((2 * width, wide + width), F32),
+            jax.ShapeDtypeStruct((2 * width, wide + 3 * width), F32),
         ),
         in_specs=[SMEM] * 4 + [VMEM] * 8,
-        out_specs=(VMEM,) * 5,
+        out_specs=(VMEM,) * 4,
         scratch_shapes=[
             pltpu.VMEM((rows_up, width), F32),
             pltpu.VMEM((peers * HUB_MOST, width), F32),
@@ -580,37 +555,29 @@
         halo, hubs, cotangent, w_self, w_neigh, bias[None, :],
     )
 
-    piece = (2 * width // PLANE, wide + width)
-    returned, hub_sum, whole = pl.pallas_call(
+    piece = (2 * width // PLANE, wide + 3 * width)
+    returned, whole = pl.pallas_call(
         backward_kernel,
         out_shape=(
             jax.ShapeDtypeStruct((peers, slots, width), BF16),
-            jax.ShapeDtypeStruct((HUB_MOST, width), F32),
             jax.ShapeDtypeStruct((PLANE,) + piece, F32),
         ),
-        in_specs=[VMEM] * 3,
-        out_specs=(VMEM,) * 3,
+        in_specs=[VMEM] * 2,
+        out_specs=(VMEM,) * 2,
         scratch_shapes=[
             pltpu.VMEM((PLANE,) + piece, BF16),
-            pltpu.VMEM((PLANE, planes, HUB_MOST, width), BF16),
             pltpu.VMEM((PLANE,) + piece, BF16),
-            pltpu.VMEM((planes, HUB_MOST, width), F32),
-            pltpu.VMEM((planes, HUB_MOST, width), F32),
             pltpu.VMEM(piece, F32),
             pltpu.VMEM((planes,) + piece, F32),
         ]
-        + [pair] * 6
-        + [pltpu.SemaphoreType.DMA((3,)), pltpu.SemaphoreType.REGULAR],
+        + [pair] * 4
+        + [pltpu.SemaphoreType.DMA((2,)), pltpu.SemaphoreType.REGULAR],
         compiler_params=pltpu.CompilerParams(
             vmem_limit_bytes=LIMIT, collective_id=1, has_side_effects=True
         ),
         name="backward_exchange",
-    )(
-        halo_back,
-        hub_back.reshape(PLANE, planes, HUB_MOST, width),
-        grads.reshape((PLANE,) + piece),
-    )
-    whole = whole.reshape(2 * width, wide + width)
+    )(halo_back, grads.reshape((PLANE,) + piece))
+    whole = whole.reshape(2 * width, wide + 3 * width)
     grad_feats = pl.pallas_call(
         final_kernel,
         out_shape=jax.ShapeDtypeStruct((local, width), BF16),
@@ -623,9 +590,9 @@
         ],
         compiler_params=params,
         name="final",
-    )(own_back, send, own, returned, hub_sum)
+    )(own_back, send, own, returned, whole)
     grad_bias = jnp.concatenate(
-        [jnp.sum(whole[8 * j : 8 * j + 8, wide:], axis=0) for j in range(wide // width)]
+        [jnp.sum(whole[8 * j : 8 * j + 8, wide : wide + width], axis=0) for j in range(wide // width)]
     )
     return (output, grad_feats, whole[:width, :wide], whole[width:, :wide], grad_bias)
 

time: 142 us -> 137 us (0.965)
  Pallas kernels: 138 us -> 132 us
    pallas_call x1, Pallas kernels: 67.1 us -> 63.4 us  [body(): pl.pallas_call(backward_kernel, out_shape=(jax.ShapeDtypeStruct((peers, s...]
    pallas_call x1, Pallas kernels: 27.7 us -> 25 us  [body(): pl.pallas_call(layer_kernel, out_shape=(jax.ShapeDtypeStruct((local, wide...]
where the time goes in v4:
time: 137 us; the launch traced here: 136 us
  Pallas kernels  132 us (96%)
  local copies, waits for them, and re-layouts  1.68 us (1%)
    pallas_call x1, Pallas kernels, body(): pl.pallas_call(backward_kernel, out_shape=(jax.ShapeDtypeStruct((peers, s...  63.4 us
    pallas_call x1, Pallas kernels, body(): pl.pallas_call(forward_kernel, out_shape=(jax.ShapeDtypeStruct((peers, sl...  31.5 us
    pallas_call x1, Pallas kernels, body(): pl.pallas_call(layer_kernel, out_shape=(jax.ShapeDtypeStruct((local, wide...  25 us
    pallas_call x1, Pallas kernels, body(): pl.pallas_call(final_kernel, out_shape=jax.ShapeDtypeStruct((local, width...  6.2 us
    pallas_call x1, Pallas kernels, body(): pl.pallas_call(gather_kernel, out_shape=(jax.ShapeDtypeStruct((peers, slo...  6 us

profile of v4, /device:TPU:2, one launch (start us, length us, event | category | flops | bytes accessed | tf_op | source)
XLA Modules:
  0.0 136.3 jit_solution(17856741409191077380)
XLA Ops:
  1.3 6.0 %gather_sent.1 = (bf16[256,8,128]{2,1,0:T(8,128)(2,1)}, bf16[8,128]{1,0:T(8,128)(2,1)}, s32[9]{0:T(128)}) custom-call(s32[368]{0:T(512)} %hub_ref.3, s32[8,256]{1,0:T(8,128)} %bitcast.18, bf16[2048,128]{1,0:T(8,128)(2,1)} %feats_ref.3), custom_call_target="tpu_custom_call" | custom-call | tf_op jit(solution)/shard_map/gather_sent/pallas_call | solution.py:500
  7.3 31.5 %forward_exchange.1 = (bf16[256,8,128]{2,1,0:T(8,128)(2,1)}, bf16[32,8,8,128]{3,2,1,0:T(8,128)(2,1)}) custom-call(bf16[256,8,128]{2,1,0:T(8,128)(2,1)} %get-tuple-element.16.sent_ref, bf16[8,128]{1,0:T(8,128)(2,1)} %get-tuple-element.17.hub_ref), custom_call_target="tpu_custom_call" | custom-call | tf_op jit(solution)/shard_map/forward_exchange/pallas_call | solution.py:517
  38.8 25.0 %layer.1 = (bf16[2048,256]{1,0:T(8,128)(2,1)}, f32[2048,128]{1,0:T(8,128)}, bf16[256,8,128]{2,1,0:T(8,128)(2,1)}, f32[256,640]{1,0:T(8,128)}) custom-call(s32[1]{0:T(128)S(6)} %copy.15.count_ref, s32[16384]{0:T(1024)} %bitcast.17, s32[16384]{0:T(1024)} %bitcast.15, s32[368]{0:T(512)} %hub_ref.3, s32[128,128]{1,0:T(8,128)} %bitcast.16, ...), custom_call_target="tpu_custom_call" | custom-call | tf_op jit(solution)/shard_map/layer/pallas_call | solution.py:534
  63.8 63.4 %backward_exchange.1 = (bf16[256,8,128]{2,1,0:T(8,128)(2,1)}, f32[32,8,640]{2,1,0:T(8,128)}) custom-call(bf16[256,8,128]{2,1,0:T(8,128)(2,1)} %get-tuple-element.23.back_ref, f32[32,8,640]{2,1,0:T(8,128)} %bitcast.13), custom_call_target="tpu_custom_call" | custom-call | tf_op jit(solution)/shard_map/backward_exchange/pallas_call | solution.py:559
  127.2 6.2 %final.1 = bf16[2048,128]{1,0:T(8,128)(2,1)} custom-call(s32[9]{0:T(128)} %get-tuple-element.21.hub_ref, s32[8,256]{1,0:T(8,128)} %bitcast.19, f32[2048,128]{1,0:T(8,128)} %get-tuple-element.22.own_ref, bf16[256,8,128]{2,1,0:T(8,128)(2,1)} %get-tuple-element.25.returned_ref, f32[256,640]{1,0:T(8,128)} %bitcast.10), custom_call_target="tpu_custom_call" | custom-call | tf_op jit(solution)/shard_map/final/pallas_call | solution.py:581
  133.4 0.7 slice_reduce_fusion.1
  134.1 1.7 %fusion = (f32[128,256]{1,0:T(8,128)}, f32[128,256]{1,0:T(8,128)}) fusion(f32[256,640]{1,0:T(8,128)} %bitcast.12), kind=kLoop, calls=%fused_computation.3 | loop fusion | bytes 524288 | tf_op jit(solution)/shard_map/slice | solution.py:597
  135.8 0.6 pad_maximum_fusion

commit v5 on v4

--- a/solution.py
+++ b/solution.py
@@ -217,8 +217,7 @@
             mean, grad, outer, preferred_element_type=F32
         )
         grad_sum = jnp.sum(grad.astype(F32).reshape(step // 8, 8, wide), axis=0)
-        for j in range(wide // width):
-            grads_ref[8 * j : 8 * j + 8, wide : wide + width] += grad_sum[:, j * width : (j + 1) * width]
+        grads_ref[2 * width - 8 :, wide:] += grad_sum
         own_ref[at, :] = lax.dot_general(grad, w_self, back, preferred_element_type=F32)
         spread[at, :] = lax.dot_general(grad, w_neigh, back, preferred_element_type=F32) * inverse
         return 0
@@ -288,14 +287,17 @@
     def hub_part(i, _):
         for j in range(2):
             at = pl.ds(pl.multiple_of(halo_end + i * 16 + j * 8, 8), 8)
-            lanes = wide + (1 + j) * width
+            lanes = wide + j * width
             grads_ref[tile(i, 8), lanes : lanes + width] = total(sums, at)
         return 0
 
     lax.fori_loop(0, hubs // 16, hub_part, 0)
 
 
-def final_kernel(hub_ref, send_ref, own_ref, returned_ref, whole_ref, out_ref, rows, parts, sums):
+def final_kernel(
+    hub_ref, send_ref, own_ref, returned_ref, whole_ref,
+    out_ref, w_self_ref, w_neigh_ref, bias_ref, rows, parts, sums,
+):
     peers, slots, width = returned_ref.shape
     local = own_ref.shape[0]
     step = 256
@@ -315,7 +317,10 @@
         return 0
 
     lax.fori_loop(0, local // step, some, 0)
-    lanes = whole_ref.shape[1] - 2 * width
+    lanes = w_self_ref.shape[1]
+    w_self_ref[...] = whole_ref[:width, :lanes]
+    w_neigh_ref[...] = whole_ref[width:, :lanes]
+    bias_ref[...] = jnp.sum(whole_ref[2 * width - 8 :, lanes:], axis=0, keepdims=True)
     for j in range(HUB_MOST):
         to = row(hub_ref[j])
         h = hub_ref[HUB_MOST] + j
@@ -537,7 +542,7 @@
             jax.ShapeDtypeStruct((local, wide), BF16),
             jax.ShapeDtypeStruct((local, width), F32),
             jax.ShapeDtypeStruct((peers, slots, width), BF16),
-            jax.ShapeDtypeStruct((2 * width, wide + 3 * width), F32),
+            jax.ShapeDtypeStruct((2 * width, 2 * wide), F32),
         ),
         in_specs=[SMEM] * 4 + [VMEM] * 8,
         out_specs=(VMEM,) * 4,
@@ -555,7 +560,7 @@
         halo, hubs, cotangent, w_self, w_neigh, bias[None, :],
     )
 
-    piece = (2 * width // PLANE, wide + 3 * width)
+    piece = (2 * width // PLANE, 2 * wide)
     returned, whole = pl.pallas_call(
         backward_kernel,
         out_shape=(
@@ -577,12 +582,17 @@
         ),
         name="backward_exchange",
     )(halo_back, grads.reshape((PLANE,) + piece))
-    whole = whole.reshape(2 * width, wide + 3 * width)
-    grad_feats = pl.pallas_call(
+    whole = whole.reshape(2 * width, 2 * wide)
+    grad_feats, grad_w_self, grad_w_neigh, grad_bias = pl.pallas_call(
         final_kernel,
-        out_shape=jax.ShapeDtypeStruct((local, width), BF16),
+        out_shape=(
+            jax.ShapeDtypeStruct((local, width), BF16),
+            jax.ShapeDtypeStruct((width, wide), F32),
+            jax.ShapeDtypeStruct((width, wide), F32),
+            jax.ShapeDtypeStruct((1, wide), F32),
+        ),
         in_specs=[SMEM] + [VMEM] * 4,
-        out_specs=VMEM,
+        out_specs=(VMEM,) * 4,
         scratch_shapes=[
             pltpu.VMEM((peers * slots, width), F32),
             pltpu.VMEM((slots, peers, width), BF16),
@@ -591,10 +601,7 @@
         compiler_params=params,
         name="final",
     )(own_back, send, own, returned, whole)
-    grad_bias = jnp.concatenate(
-        [jnp.sum(whole[8 * j : 8 * j + 8, wide : wide + width], axis=0) for j in range(wide // width)]
-    )
-    return (output, grad_feats, whole[:width, :wide], whole[width:, :wide], grad_bias)
+    return (output, grad_feats, grad_w_self, grad_w_neigh, grad_bias[0])
 
 
 def solution(mesh):

time: 137 us -> 130 us (0.949)
  Pallas kernels: 132 us -> 129 us
  local copies, waits for them, and re-layouts: 1.68 us -> 0 us
    pallas_call x1, Pallas kernels: 63.4 us -> 33.9 us  [body(): pl.pallas_call(backward_kernel, out_shape=(jax.ShapeDtypeStruct((peers, s...]
    pallas_call x1, Pallas kernels: 25 us -> 51 us  [body(): pl.pallas_call(layer_kernel, out_shape=(jax.ShapeDtypeStruct((local, wide...]
    slice x1 -> x0, local copies, waits for them, and re-layouts: 1.68 us -> none  [body(): whole[width:, :wide]]
where the time goes in v5:
time: 130 us
  Pallas kernels  129 us (99%)
  between operations  1.3 us (1%)
    pallas_call x1, Pallas kernels, body(): pl.pallas_call(layer_kernel, out_shape=(jax.ShapeDtypeStruct((local, wide...  51 us
    pallas_call x1, Pallas kernels, body(): pl.pallas_call(backward_kernel, out_shape=(jax.ShapeDtypeStruct((peers, s...  33.9 us
    pallas_call x1, Pallas kernels, body(): pl.pallas_call(forward_kernel, out_shape=(jax.ShapeDtypeStruct((peers, sl...  31.5 us
    pallas_call x1, Pallas kernels, body(): pl.pallas_call(final_kernel, out_shape=(jax.ShapeDtypeStruct((local, widt...  6.24 us
    pallas_call x1, Pallas kernels, body(): pl.pallas_call(gather_kernel, out_shape=(jax.ShapeDtypeStruct((peers, slo...  6 us

profile of v5, /device:TPU:2, one launch (start us, length us, event | category | flops | bytes accessed | tf_op | source)
XLA Modules:
  0.0 129.9 jit_solution(3350082761028968853)
XLA Ops:
  1.3 6.0 %gather_sent.1 = (bf16[256,8,128]{2,1,0:T(8,128)(2,1)}, bf16[8,128]{1,0:T(8,128)(2,1)}, s32[9]{0:T(128)}) custom-call(s32[368]{0:T(512)} %hub_ref.3, s32[8,256]{1,0:T(8,128)} %bitcast.17, bf16[2048,128]{1,0:T(8,128)(2,1)} %feats_ref.3), custom_call_target="tpu_custom_call" | custom-call | tf_op jit(solution)/shard_map/gather_sent/pallas_call | solution.py:505
  7.3 31.5 %forward_exchange.1 = (bf16[256,8,128]{2,1,0:T(8,128)(2,1)}, bf16[32,8,8,128]{3,2,1,0:T(8,128)(2,1)}) custom-call(bf16[256,8,128]{2,1,0:T(8,128)(2,1)} %get-tuple-element.20.sent_ref, bf16[8,128]{1,0:T(8,128)(2,1)} %get-tuple-element.21.hub_ref), custom_call_target="tpu_custom_call" | custom-call | tf_op jit(solution)/shard_map/forward_exchange/pallas_call | solution.py:522
  38.8 51.0 %layer.1 = (bf16[2048,256]{1,0:T(8,128)(2,1)}, f32[2048,128]{1,0:T(8,128)}, bf16[256,8,128]{2,1,0:T(8,128)(2,1)}, f32[256,512]{1,0:T(8,128)}) custom-call(s32[1]{0:T(128)S(6)} %copy.15.count_ref, s32[16384]{0:T(1024)} %bitcast.16, s32[16384]{0:T(1024)} %bitcast.14, s32[368]{0:T(512)} %hub_ref.3, s32[128,128]{1,0:T(8,128)} %bitcast.15, ...), custom_call_target="tpu_custom_call" | custom-call | tf_op jit(solution)/shard_map/layer/pallas_call | solution.py:539
  89.7 33.9 %backward_exchange.1 = (bf16[256,8,128]{2,1,0:T(8,128)(2,1)}, f32[32,8,512]{2,1,0:T(8,128)}) custom-call(bf16[256,8,128]{2,1,0:T(8,128)(2,1)} %get-tuple-element.27.back_ref, f32[32,8,512]{2,1,0:T(8,128)} %bitcast.12), custom_call_target="tpu_custom_call" | custom-call | tf_op jit(solution)/shard_map/backward_exchange/pallas_call | solution.py:564
  123.6 6.2 %final.1 = (bf16[2048,128]{1,0:T(8,128)(2,1)}, f32[128,256]{1,0:T(8,128)}, f32[128,256]{1,0:T(8,128)}, f32[1,256]{1,0:T(1,128)}) custom-call(s32[9]{0:T(128)} %get-tuple-element.25.hub_ref, s32[8,256]{1,0:T(8,128)} %bitcast.18, f32[2048,128]{1,0:T(8,128)} %get-tuple-element.26.own_ref, bf16[256,8,128]{2,1,0:T(8,128)(2,1)} %get-tuple-element.29.returned_ref, ...), custom_call_target="tpu_custom_call" | custom-call | tf_op jit(solution)/shard_map/final/pallas_call | solution.py:586
